TPU v7x, 32 devices: a whole 2x2x4 slice. The times are simulated.
32 devices in a mesh: lon: 8 (over z, x), lat: 4 (over y, core).
Axes of the slice: x: 2, y: 2, z: 4, core: 2. Of those that a mesh axis runs over, the one named last changes fastest.
Arguments:
- tracers: float32 [40, 8, 32, 1024], P(None, None, 'lat', 'lon'), may hold values from -6 to 6
- kmt: int32 [32, 1024], P('lat', 'lon'), may hold values from 0 to 8
Outputs:
- updated: float32 [40, 8, 32, 1024], P(None, None, 'lat', 'lon')
Inputs may be any that keep to these rules, and one draw needn't show every extreme that they name: Level k of column (j, i) is ocean exactly when k < kmt[j, i].
All inputs are finite; a program needn't handle non-finite values.
Results may differ from a plain program's by a relative error of at most 0.00002.
Values sent between devices are 32-bit elements; how exact they have to be, the bound alone decides.
No kernel may reach another device: no remote copies, remote signals or barrier semaphores. Data moves between devices by JAX's collectives and lax.ppermute only.
A program may use at most 64 MiB of HBM per device.

v0:
```python
import jax
import jax.numpy as jnp
from jax import lax
from jax.sharding import PartitionSpec as P

THERMAL = 0.2
HALINE = 0.8
REDI_COEF = 0.1
SKEW_COEF = 0.05
SLOPE_MAX = 0.6
SLOPE_WIDTH = 0.2


def padded(block, sides, width, periodic):
    for axis, dim in sides:
        count = lax.axis_size(axis)
        forward = [(i, i + 1) for i in range(count - 1)]
        if periodic:
            forward.append((count - 1, 0))
        backward = [(target, source) for source, target in forward]
        low = lax.ppermute(
            lax.slice_in_dim(block, block.shape[dim] - width, None, axis=dim), axis, forward
        )
        high = lax.ppermute(lax.slice_in_dim(block, 0, width, axis=dim), axis, backward)
        block = jnp.concatenate([low, block, high], axis=dim)
    return block


def from_partner(value, axis, apart):
    mask = 2**apart
    pairs = [(source, source ^ mask) for source in range(lax.axis_size(axis))]
    return lax.ppermute(value, axis, pairs)


def taper(slope):
    return slope * 0.5 * (1.0 + jnp.tanh((SLOPE_MAX - jnp.abs(slope)) / SLOPE_WIDTH))


def pad_levels(values):
    zero_layer = jnp.zeros_like(values[..., :1, :, :])
    return jnp.concatenate([zero_layer, values, zero_layer], axis=-3)


def slope_fields(density, wet_mask):
    level_mask = wet_mask[1:] * wet_mask[:-1]
    strat = (density[1:] - density[:-1]) * level_mask
    strat_pad = pad_levels(strat)
    strat_cell = 0.5 * (strat_pad[:-1] + strat_pad[1:])
    east_mask = wet_mask[:, 1:-1, :-1] * wet_mask[:, 1:-1, 1:]
    north_mask = wet_mask[:, :-1, 1:-1] * wet_mask[:, 1:, 1:-1]
    grad_east = (density[:, 1:-1, 1:] - density[:, 1:-1, :-1]) * east_mask
    strat_east = 0.5 * (strat_cell[:, 1:-1, 1:] + strat_cell[:, 1:-1, :-1])
    slope_x = taper(grad_east / jnp.maximum(strat_east, 1.0))
    grad_north = (density[:, 1:, 1:-1] - density[:, :-1, 1:-1]) * north_mask
    strat_north = 0.5 * (strat_cell[:, 1:, 1:-1] + strat_cell[:, :-1, 1:-1])
    slope_y = taper(grad_north / jnp.maximum(strat_north, 1.0))
    cell_x = 0.5 * (slope_x[..., :-1] + slope_x[..., 1:])
    cell_y = 0.5 * (slope_y[:, :-1, :] + slope_y[:, 1:, :])
    level_x = 0.5 * (cell_x[:-1] + cell_x[1:])
    level_y = 0.5 * (cell_y[:-1] + cell_y[1:])
    return (level_mask, east_mask, north_mask, slope_x, slope_y, level_x, level_y)


def tracer_step(field, fields):
    level_mask, east_mask, north_mask, slope_x, slope_y, level_x, level_y = fields
    vert_diff = (field[..., 1:, :, :] - field[..., :-1, :, :]) * level_mask
    vert_pad = pad_levels(vert_diff)
    vert_cell = 0.5 * (vert_pad[..., :-1, :, :] + vert_pad[..., 1:, :, :])
    grad_x = (field[..., 1:-1, 1:] - field[..., 1:-1, :-1]) * east_mask
    grad_y = (field[..., 1:, 1:-1] - field[..., :-1, 1:-1]) * north_mask
    flux_x = (
        -(
            REDI_COEF * grad_x
            + (REDI_COEF - SKEW_COEF)
            * slope_x
            * 0.5
            * (vert_cell[..., 1:-1, 1:] + vert_cell[..., 1:-1, :-1])
        )
        * east_mask
    )
    flux_y = (
        -(
            REDI_COEF * grad_y
            + (REDI_COEF - SKEW_COEF)
            * slope_y
            * 0.5
            * (vert_cell[..., 1:, 1:-1] + vert_cell[..., :-1, 1:-1])
        )
        * north_mask
    )
    cell_gx = 0.5 * (grad_x[..., :-1] + grad_x[..., 1:])
    cell_gy = 0.5 * (grad_y[..., :-1, :] + grad_y[..., 1:, :])
    level_gx = 0.5 * (cell_gx[..., :-1, :, :] + cell_gx[..., 1:, :, :])
    level_gy = 0.5 * (cell_gy[..., :-1, :, :] + cell_gy[..., 1:, :, :])
    flux_z = (
        -(
            (REDI_COEF + SKEW_COEF) * (level_x * level_gx + level_y * level_gy)
            + REDI_COEF * (level_x * level_x + level_y * level_y) * vert_diff[..., 1:-1, 1:-1]
        )
        * level_mask[:, 1:-1, 1:-1]
    )
    flux_pad = pad_levels(flux_z)
    tendency = -(
        flux_x[..., 1:]
        - flux_x[..., :-1]
        + (flux_y[..., 1:, :] - flux_y[..., :-1, :])
        + (flux_pad[..., 1:, :, :] - flux_pad[..., :-1, :, :])
    )
    return field[..., 1:-1, 1:-1] + tendency


def local(tracers, kmt):
    channels = tracers.shape[0]
    levels = tracers.shape[1]
    rows_here = tracers.shape[2]
    level_index = lax.broadcasted_iota(jnp.int32, (levels,) + kmt.shape, 0)
    wet_mask = (level_index < kmt[None]).astype(jnp.float32)
    stacked = jnp.concatenate([tracers, wet_mask[None]], axis=0)
    lat_index = lax.axis_index("lat")
    at_top = lat_index == lax.axis_size("lat") - 1
    lon_wide = padded(stacked, (("lon", 3),), 1, True)
    extended = padded(lon_wide, (("lat", 2),), 1, False)
    edge_row = stacked[:, :, rows_here - 1, :]
    partner = edge_row
    for bit_index in range(lax.axis_size("lon").bit_length() - 1):
        partner = from_partner(partner, "lon", bit_index)
    mirrored = partner[..., ::-1]
    north_row = jnp.where(at_top, mirrored, extended[:, :, rows_here + 1, 1:-1])
    extended = extended.at[:, :, rows_here + 1, 1:-1].set(north_row)
    density = HALINE * extended[1] - THERMAL * extended[0]
    fields = slope_fields(density, extended[channels])
    return tracer_step(extended[:channels], fields)


def solution(mesh):
    return jax.shard_map(
        local,
        mesh=mesh,
        in_specs=(P(None, None, "lat", "lon"), P("lat", "lon")),
        out_specs=P(None, None, "lat", "lon"),
        check_vma=False,
    )
```

profile of v0, /device:TPU:0, one launch (start us, length us, event | category | flops | bytes accessed | tf_op | source)
XLA Modules:
  0.0 58.4 jit_solution(1578023485517045898)
XLA Ops:
  0.0 1.6 %copy.14 = f32[40,8,8,128]{3,1,0,2:T(8,128)S(1)} copy(f32[40,8,8,128]{3,2,1,0:T(8,128)} %param.4) | data formatting | bytes 2621440 | tf_op args[0]
  1.6 3.0 %collective-permute-start.4 = (f32[41,8,128]{2,1,0:T(8,128)S(1)}, f32[41,8,128]{2,1,0:T(8,128)}, u32[]{:S(2)}, u32[]{:S(2)}) collective-permute-start(f32[41,8,128]{2,1,0:T(8,128)S(1)} %fusion.28), channel_id=1, source_target_pairs={{0,4},{4,0},{8,12},{12,8},{16,20},{20,16},{24,28},{28,24},{1,5},{5... | collective-permute-start | bytes 503816 | tf_op jit(solution)/shard_map/ppermute | solution.py:32
  4.7 1.5 %fusion.12 = (f32[41,8,8,1]{3,1,0,2:T(8,128)}, f32[41,8,8,1]{3,1,0,2:T(8,128)S(1)}) fusion(f32[1,8,8,128]{3,1,0,2:T(8,128)S(1)} %fusion.43, f32[40,8,8,128]{3,1,0,2:T(8,128)S(1)} %copy.14), kind=kLoop, calls=%fused_computation.21 | loop fusion | flops 5248 | bytes 1364480 | tf_op jit(solution)/shard_map/concatenate | solution.py:118
  6.2 1.9 %copy.15 = f32[41,8,8,1]{0,2,3,1:T(8,128)S(1)} copy(f32[41,8,8,1]{3,1,0,2:T(8,128)} %get-tuple-element.33) | data formatting | bytes 20992 | tf_op jit(solution)/shard_map/slice | solution.py:22
  8.1 0.7 %copy.16 = f32[41,8,8,1]{0,2,3,1:T(8,128)S(1)} copy(f32[41,8,8,1]{3,1,0,2:T(8,128)S(1)} %get-tuple-element.34) | data formatting | bytes 20992 | tf_op jit(solution)/shard_map/slice | solution.py:24
  8.8 4.7 %collective-permute-start.1 = (f32[41,8,8,1]{0,2,3,1:T(8,128)S(1)}, f32[41,8,8,1]{0,2,3,1:T(8,128)S(1)}, u32[]{:S(2)}, u32[]{:S(2)}) collective-permute-start(f32[41,8,8,1]{0,2,3,1:T(8,128)S(1)} %copy.16), channel_id=1, source_target_pairs={{4,0},{8,4},{12,8},{16,12},{20,16},{24,20},{28,24},{0,28},{5,1},{9... | collective-permute-start | bytes 31496 | tf_op jit(solution)/shard_map/ppermute | solution.py:24
  13.5 1.2 %collective-permute-done = f32[41,8,8,1]{0,2,3,1:T(8,128)S(1)} collective-permute-done((f32[41,8,8,1]{0,2,3,1:T(8,128)S(1)}, f32[41,8,8,1]{0,2,3,1:T(8,128)S(1)}, u32[]{:S(2)}, u32[]{:S(2)}) %collective-permute-start) | collective-permute-done | bytes 10528 | tf_op jit(solution)/shard_map/ppermute | solution.py:21
  15.4 1.7 %copy.18 = f32[41,8,8,1]{3,1,0,2:T(8,128)} copy(f32[41,8,8,1]{0,2,3,1:T(8,128)S(1)} %collective-permute-done.1) | data formatting | bytes 20992 | tf_op jit(solution)/shard_map/ppermute | solution.py:24
  17.1 2.0 %pad_maximum_fusion.4 = (f32[41,8,1,130]{3,1,0,2:T(8,128)S(1)}, f32[41,8,1,130]{3,1,0,2:T(8,128)}) fusion(f32[41,8,8,1]{3,1,0,2:T(8,128)} %copy.18, f32[41,8,8,1]{3,1,0,2:T(8,128)S(1)} %copy.17, f32[1,8,8,128]{3,1,0,2:T(8,128)S(1)} %fusion.43, f32[40,8,8,128]{3,1,0,2:T(8,128)S(1)} %copy.14), kind=kLoop, calls=%fused_computation.45 | loop fusion | flops 255840 | bytes 1705600 | tf_op jit(solution)/shard_map/slice | solution.py:22
  19.2 1.3 %collective-permute-start.3 = (f32[41,8,1,130]{3,1,0,2:T(8,128)}, f32[41,8,1,130]{3,1,0,2:T(8,128)S(1)}, u32[]{:S(2)}, u32[]{:S(2)}) collective-permute-start(f32[41,8,1,130]{3,1,0,2:T(8,128)} %get-tuple-element.30), channel_id=1, source_target_pairs={{1,0},{2,1},{3,2},{5,4},{6,5},{7,6},{9,8},{10,9},{11,10},{13,12},{... | collective-permute-start | bytes 511688 | tf_op jit(solution)/shard_map/ppermute | solution.py:24
  20.4 3.8 %collective-permute-start.2 = (f32[41,8,1,130]{3,1,0,2:T(8,128)S(1)}, f32[41,8,1,130]{3,1,0,2:T(8,128)}, u32[]{:S(2)}, u32[]{:S(2)}) collective-permute-start(f32[41,8,1,130]{3,1,0,2:T(8,128)S(1)} %get-tuple-element.29), channel_id=1, source_target_pairs={{0,1},{1,2},{2,3},{4,5},{5,6},{6,7},{8,9},{9,10},{10,11},{12,13},{... | collective-permute-start | bytes 511688 | tf_op jit(solution)/shard_map/ppermute | solution.py:21
  24.2 7.2 %collective-permute-done.5 = f32[41,8,128]{2,1,0:T(8,128)} collective-permute-done((f32[41,8,128]{2,1,0:T(8,128)}, f32[41,8,128]{2,1,0:T(8,128)}, u32[]{:S(2)}, u32[]{:S(2)}) %collective-permute-start.5) | collective-permute-done | bytes 167968 | tf_op jit(solution)/shard_map/ppermute | solution.py:32
  31.4 1.0 %collective-permute-start.6 = (f32[41,8,128]{2,1,0:T(8,128)}, f32[41,8,128]{2,1,0:T(8,128)S(1)}, u32[]{:S(2)}, u32[]{:S(2)}) collective-permute-start(f32[41,8,128]{2,1,0:T(8,128)} %collective-permute-done.5), channel_id=1, source_target_pairs={{0,16},{4,20},{8,24},{12,28},{16,0},{20,4},{24,8},{28,12},{1,17},{... | collective-permute-start | bytes 503816 | tf_op jit(solution)/shard_map/ppermute | solution.py:32
  32.4 0.7 %copy-done = f32[41,8,1,130]{3,1,0,2:T(8,128)} copy-done((f32[41,8,1,130]{3,1,0,2:T(8,128)}, f32[41,8,1,130]{3,1,0,2:T(8,128)S(1)}, u32[]{:S(2)}) %copy-start) | copy-done | bytes 170584
  33.1 2.5 %pad_maximum_fusion = f32[41,8,10,130]{3,1,0,2:T(8,128)S(1)} fusion(f32[41,8,1,130]{3,1,0,2:T(8,128)S(1)} %collective-permute-done.3, f32[41,8,8,1]{3,1,0,2:T(8,128)} %copy.18, f32[1,8,8,128]{3,1,0,2:T(8,128)S(1)} %fusion.43, f32[40,8,8,128]{3,1,0,2:T(8,128)S(1)} %copy.14, f32[41,8,8,1]{3,1,0,2:T(8,128)S(1)} %copy.17, f32[41,8,1,130]{3,1,0,2:T(8,128)} %collective-permute-done.2), kind=kLoop, calls=%fused_computation | loop fusion | flops 2132000 | bytes 3411200 | tf_op jit(solution)/shard_map/concatenate | solution.py:25
  36.0 6.1 %collective-permute-done.6 = f32[41,8,128]{2,1,0:T(8,128)S(1)} collective-permute-done((f32[41,8,128]{2,1,0:T(8,128)}, f32[41,8,128]{2,1,0:T(8,128)S(1)}, u32[]{:S(2)}, u32[]{:S(2)}) %collective-permute-start.6) | collective-permute-done | bytes 167968 | tf_op jit(solution)/shard_map/ppermute | solution.py:32
  42.1 0.8 %rev.3 = f32[41,8,128]{2,1,0:T(8,128)} reverse(f32[41,8,128]{2,1,0:T(8,128)S(1)} %collective-permute-done.6), dimensions={2} | reverse | bytes 335872 | tf_op jit(solution)/shard_map/rev | solution.py:127
  42.9 1.1 %fusion.27 = f32[41,8,1,128]{3,1,2,0:T(8,128)S(1)} fusion(f32[41,8,128]{2,1,0:T(8,128)} %rev.3, f32[41,8,1,130]{3,1,0,2:T(8,128)} %copy-done, pred[]{:T(512)S(6)} %eq.3), kind=kLoop, calls=%fused_computation.48 | loop fusion | flops 41984 | bytes 503809 | tf_op jit(solution)/shard_map/reshape.27
  44.0 6.2 %scatter.4 = f32[41,8,10,130]{3,1,2,0:T(8,128)S(1)} dynamic-update-slice(f32[41,8,10,130]{3,1,2,0:T(8,128)S(1)} %copy.19, f32[41,8,1,128]{3,1,2,0:T(8,128)S(1)} %fusion.27, s32[]{:T(128)} %constant.68.clone.1, s32[]{:T(128)} %constant.68.clone.1, s32[]{:T(128)} %constant.69.clone.1, s32[]{:T(128)} %constant.70.clone.1) | dynamic-update-slice | bytes 335876 | tf_op jit(solution)/shard_map/scatter | solution.py:129
  51.8 1.5 %fusion.4 = (f32[40,8,8,129]{3,1,2,0:T(8,128)S(1)}, f32[40,8,8,129]{3,1,2,0:T(8,128)S(1)}) fusion(f32[40,8,10,130]{3,1,2,0:T(8,128)S(1)} %add_multiply_fusion, f32[8,8,129]{2,0,1:T(8,128)S(1)} %get-tuple-element.19, f32[8,8,129]{2,0,1:T(8,128)S(1)} %get-tuple-element.21, f32[41,8,10,130]{3,1,2,0:T(8,128)S(1)} %scatter.4), kind=kLoop, calls=%fused_computation.8 | loop fusion | flops 2641920 | bytes 7991808 | tf_op jit(solution)/shard_map/mul | solution.py:72
  53.3 1.6 %fusion.9 = (f32[40,8,9,128]{3,1,2,0:T(8,128)S(1)}, f32[40,8,9,128]{3,1,2,0:T(8,128)S(1)}) fusion(f32[40,8,10,130]{3,1,2,0:T(8,128)S(1)} %add_multiply_fusion, f32[8,9,128]{2,0,1:T(8,128)S(1)} %get-tuple-element.24, f32[8,9,128]{2,0,1:T(8,128)S(1)} %get-tuple-element.26, f32[41,8,10,130]{3,1,2,0:T(8,128)S(1)} %scatter.4), kind=kLoop, calls=%fused_computation.17 | loop fusion | flops 2949120 | bytes 8921088 | tf_op jit(solution)/shard_map/mul | solution.py:82
  55.4 0.7 %fusion.15 = f32[40,7,8,128]{3,1,2,0:T(8,128)S(1)} fusion(f32[40,7,10,130]{3,1,2,0:T(8,128)S(1)} %fusion, f32[40,8,8,128]{3,1,2,0:T(8,128)S(1)} %get-tuple-element.40, f32[40,8,8,128]{3,1,2,0:T(8,128)S(1)} %get-tuple-element.41, f32[7,8,128]{2,0,1:T(8,128)S(1)} %slice.345, f32[7,8,128]{2,0,1:T(8,128)S(1)} %get-tuple-element.36, ...), kind=kLoop, calls=%fused_computation.25 | loop fusion | flops 2867200 | bytes 6995968 | tf_op jit(solution)/shard_map/mul | solution.py:96
  56.1 0.9 %fusion.25 = f32[40,8,8,128]{3,1,2,0:T(8,128)S(1)} fusion(f32[40,8,9,128]{3,1,2,0:T(8,128)S(1)} %get-tuple-element.22, f32[40,8,8,129]{3,1,2,0:T(8,128)S(1)} %get-tuple-element.17, f32[41,8,10,130]{3,1,2,0:T(8,128)S(1)} %scatter.4, f32[40,7,8,128]{3,1,2,0:T(8,128)S(1)} %fusion.15), kind=kLoop, calls=%fused_computation.40 | loop fusion | flops 2293760 | bytes 9011200 | tf_op jit(solution)/shard_map/add | solution.py:109
  57.0 1.3 %copy.20 = f32[40,8,8,128]{3,2,1,0:T(8,128)} copy(f32[40,8,8,128]{3,1,2,0:T(8,128)S(1)} %fusion.25) | data formatting | bytes 2621440 | tf_op jit(solution)/shard_map/add | solution.py:109
  (24 shorter events, 3.3 us)
Async XLA Ops:
  0.0 1.6 %copy-start.1 = (s32[8,128]{1,0:T(8,128)S(1)}, s32[8,128]{1,0:T(8,128)}, u32[]{:S(2)}) copy-start(s32[8,128]{1,0:T(8,128)} %param.5) | copy-start | bytes 12292
  1.6 22.6 %collective-permute-start.4 = (f32[41,8,128]{2,1,0:T(8,128)S(1)}, f32[41,8,128]{2,1,0:T(8,128)}, u32[]{:S(2)}, u32[]{:S(2)}) collective-permute-start(f32[41,8,128]{2,1,0:T(8,128)S(1)} %fusion.28), channel_id=1, source_target_pairs={{0,4},{4,0},{8,12},{12,8},{16,20},{20,16},{24,28},{28,24},{1,5},{5... | collective-permute-start | bytes 503816 | tf_op jit(solution)/shard_map/ppermute | solution.py:32
  8.1 6.6 %collective-permute-start = (f32[41,8,8,1]{0,2,3,1:T(8,128)S(1)}, f32[41,8,8,1]{0,2,3,1:T(8,128)S(1)}, u32[]{:S(2)}, u32[]{:S(2)}) collective-permute-start(f32[41,8,8,1]{0,2,3,1:T(8,128)S(1)} %copy.15), channel_id=1, source_target_pairs={{0,4},{4,8},{8,12},{12,16},{16,20},{20,24},{24,28},{28,0},{1,5},{5... | collective-permute-start | bytes 31496 | tf_op jit(solution)/shard_map/ppermute | solution.py:21
  8.8 6.6 %collective-permute-start.1 = (f32[41,8,8,1]{0,2,3,1:T(8,128)S(1)}, f32[41,8,8,1]{0,2,3,1:T(8,128)S(1)}, u32[]{:S(2)}, u32[]{:S(2)}) collective-permute-start(f32[41,8,8,1]{0,2,3,1:T(8,128)S(1)} %copy.16), channel_id=1, source_target_pairs={{4,0},{8,4},{12,8},{16,12},{20,16},{24,20},{28,24},{0,28},{5,1},{9... | collective-permute-start | bytes 31496 | tf_op jit(solution)/shard_map/ppermute | solution.py:24
  19.2 13.2 %collective-permute-start.3 = (f32[41,8,1,130]{3,1,0,2:T(8,128)}, f32[41,8,1,130]{3,1,0,2:T(8,128)S(1)}, u32[]{:S(2)}, u32[]{:S(2)}) collective-permute-start(f32[41,8,1,130]{3,1,0,2:T(8,128)} %get-tuple-element.30), channel_id=1, source_target_pairs={{1,0},{2,1},{3,2},{5,4},{6,5},{7,6},{9,8},{10,9},{11,10},{13,12},{... | collective-permute-start | bytes 511688 | tf_op jit(solution)/shard_map/ppermute | solution.py:24
  20.4 11.9 %collective-permute-start.2 = (f32[41,8,1,130]{3,1,0,2:T(8,128)S(1)}, f32[41,8,1,130]{3,1,0,2:T(8,128)}, u32[]{:S(2)}, u32[]{:S(2)}) collective-permute-start(f32[41,8,1,130]{3,1,0,2:T(8,128)S(1)} %get-tuple-element.29), channel_id=1, source_target_pairs={{0,1},{1,2},{2,3},{4,5},{5,6},{6,7},{8,9},{9,10},{10,11},{12,13},{... | collective-permute-start | bytes 511688 | tf_op jit(solution)/shard_map/ppermute | solution.py:21
  24.2 7.2 %collective-permute-start.5 = (f32[41,8,128]{2,1,0:T(8,128)}, f32[41,8,128]{2,1,0:T(8,128)}, u32[]{:S(2)}, u32[]{:S(2)}) collective-permute-start(f32[41,8,128]{2,1,0:T(8,128)} %collective-permute-done.4), channel_id=1, source_target_pairs={{0,8},{4,12},{8,0},{12,4},{16,24},{20,28},{24,16},{28,20},{1,9},{5... | collective-permute-start | bytes 503816 | tf_op jit(solution)/shard_map/ppermute | solution.py:32
  31.4 10.7 %collective-permute-start.6 = (f32[41,8,128]{2,1,0:T(8,128)}, f32[41,8,128]{2,1,0:T(8,128)S(1)}, u32[]{:S(2)}, u32[]{:S(2)}) collective-permute-start(f32[41,8,128]{2,1,0:T(8,128)} %collective-permute-done.5), channel_id=1, source_target_pairs={{0,16},{4,20},{8,24},{12,28},{16,0},{20,4},{24,8},{28,12},{1,17},{... | collective-permute-start | bytes 503816 | tf_op jit(solution)/shard_map/ppermute | solution.py:32
  32.3 0.7 %copy-start = (f32[41,8,1,130]{3,1,0,2:T(8,128)}, f32[41,8,1,130]{3,1,0,2:T(8,128)S(1)}, u32[]{:S(2)}) copy-start(f32[41,8,1,130]{3,1,0,2:T(8,128)S(1)} %collective-permute-done.3) | copy-start | bytes 511684
where the time goes:
time: 58.6 us; the launch traced here: 58.4 us
  local copies, waits for them, and re-layouts  16 us (27%)
  waiting for transfers between devices  14.4 us (25%)
  other arithmetic  13.9 us (24%)
  starting transfers between devices  13.8 us (24%)
    ppermute x3, waiting for transfers between devices, from_partner(): return lax.ppermute(value, axis, pairs)  13.2 us
    scatter x1, local copies, waits for them, and re-layouts, local(): extended = extended.at[:, :, rows_here + 1, 1:-1].set(north_row)  6.16 us
    ppermute x2, starting transfers between devices, padded(): lax.ppermute(lax.slice_in_dim(block, 0, width, axis=dim), axis, backward)  6.03 us
    ppermute x3, starting transfers between devices, from_partner(): return lax.ppermute(value, axis, pairs)  3.99 us
    ppermute x2, starting transfers between devices, padded(): lax.ppermute(lax.slice_in_dim(block, block.shape[dim] - width, None, axis...  3.82 us
    concatenate x1, other arithmetic, padded(): block = jnp.concatenate([low, block, high], axis=dim)  2.49 us
    unnamed x5, local copies, waits for them, and re-layouts  2.31 us
    slice x1, other arithmetic, padded(): lax.slice_in_dim(block, block.shape[dim] - width, None, axis=dim)  2.04 us
  transfers between devices with their start and end apart: 7, of which 3 were waited for; matrix products, arithmetic and copies ran while one was open for 20% of the time, Pallas kernels for 0%

commit v1 on v0

v1 whole, which is shorter than its diff:
```python
import functools

import jax
import jax.numpy as jnp
from jax import lax
from jax.experimental import pallas as pl
from jax.experimental.pallas import tpu as pltpu
from jax.sharding import PartitionSpec as P

THERMAL = 0.2
HALINE = 0.8
REDI = 0.1
SKEW = 0.05
SLOPE_MAX = 0.6
SLOPE_WIDTH = 0.2
FACE = 0.25 * (REDI - SKEW)
LEVEL = 0.25 * (REDI + SKEW) / REDI
CHUNKS = 5


def taper(slope):
    return slope * 0.5 * (1.0 + jnp.tanh((SLOPE_MAX - jnp.abs(slope)) * (1.0 / SLOPE_WIDTH)))


def lanes_of(shape):
    return lax.broadcasted_iota(jnp.int32, shape, len(shape) - 1)


def rows_of(shape):
    return lax.broadcasted_iota(jnp.int32, shape, len(shape) - 2)


def density_of(heat, salt):
    return HALINE * salt - THERMAL * heat


def as_mask(flag):
    return jnp.where(flag, 1.0, 0.0)


def slope_at(here, there, mask, strat_here, strat_there):
    return taper((here - there) * mask / jnp.maximum(0.5 * (strat_here + strat_there), 1.0))


def level_lists(values, masks):
    diffs = [(values[k + 1] - values[k]) * masks[k] for k in range(len(values) - 1)]
    sums = [diffs[0]] + [a + b for a, b in zip(diffs, diffs[1:])] + [diffs[-1]]
    return diffs, sums


def level_rows(values, mask):
    diffs = (pltpu.roll(values, values.shape[0] - 1, 0) - values) * mask
    return diffs, diffs + pltpu.roll(diffs, 1, 0)


def pack_kernel(dims, info, x_hbm, kmt_ref, x_ref, east_ref, west_ref, even_ref, odd_ref, sems):
    nt, nz, rows, cols, mirror_color = dims
    per = cols // nt
    step = nt // CHUNKS
    copies = []
    for c in range(CHUNKS):
        part = pl.ds(c * step * nz * rows, step * nz * rows)
        copies.append(pltpu.make_async_copy(x_hbm.at[part], x_ref.at[part], sems.at[c]))
        copies[-1].start()
    lane = lanes_of((rows, cols))
    odd, top = info[0] == 1, info[1] == 1
    kmt = kmt_ref[...].astype(jnp.float32)
    packs = nz // per + 1
    east, west = [jnp.zeros((rows, cols), jnp.float32)] * packs, [jnp.zeros((rows, cols), jnp.float32)] * packs
    spot = (nz % per) * nt
    last = (lane >= spot) & (lane < spot + nt)
    east[-1] = jnp.where(last, jnp.broadcast_to(kmt[:, cols - 1 :], (rows, cols)), 0.0)
    west[-1] = jnp.where(last, jnp.broadcast_to(kmt[:, :1], (rows, cols)), 0.0)

    def put_rows(low, high, start):
        count = low.shape[0]
        index = lanes_of((count, cols))
        turned = jnp.take_along_axis(high, jnp.where(top, cols - 1 - index, index), axis=1, mode="promise_in_bounds")
        refs = (even_ref, odd_ref)
        for color in (0, 1):
            up = turned if color == mirror_color else high
            goes_up = odd if color == 1 else jnp.logical_not(odd)
            refs[color][pl.ds(start, count), :] = jnp.where(goes_up, up, low)

    put_rows(jnp.broadcast_to(kmt[:1], (nz, cols)), jnp.broadcast_to(kmt[rows - 1 :], (nz, cols)), nt * nz)
    for c in range(CHUNKS):
        copies[c].wait()
        for t in range(c * step, (c + 1) * step):
            for k in range(nz):
                value = x_ref[pl.ds((t * nz + k) * rows, rows), :]
                spot = (k % per) * nt + t
                here = lane == spot
                east[k // per] = jnp.where(here, pltpu.roll(value, (spot + 1) % cols, 1), east[k // per])
                west[k // per] = jnp.where(here, pltpu.roll(value, spot, 1), west[k // per])
            low = x_ref[pl.ds(t * nz * rows, nz, stride=rows), :]
            high = x_ref[pl.ds(t * nz * rows + rows - 1, nz, stride=rows), :]
            put_rows(low, high, t * nz)
    for i in range(packs):
        east_ref[pl.ds(i * rows, rows), :] = east[i]
        west_ref[pl.ds(i * rows, rows), :] = west[i]


def main_kernel(dims, info, x_ref, kmt_ref, own_east, own_west, from_west, from_east, even_ref, odd_ref, out_hbm,
                out_ref, ax_ref, bx_ref, ay_ref, by_ref, wm_ref, p_ref, q_ref, z_ref, side_ref, sems):
    nt, nz, rows, cols, _ = dims
    per = cols // nt
    half = cols // 2
    shape = (rows, cols)
    lane, row = lanes_of(shape), rows_of(shape)
    odd, bottom = info[0] == 1, info[2] == 1
    kmt = kmt_ref[...].astype(jnp.float32)

    left = lane < half

    def pair(west, east, k):
        start = (k % per) * nt
        part = pl.ds((k // per) * rows, rows)
        return jnp.where(left, pltpu.roll(west[part, :], (cols - start) % cols, 1), pltpu.roll(east[part, :], (half - start) % cols, 1))

    def both(west, east):
        return jnp.where(left, jnp.broadcast_to(west, shape), jnp.broadcast_to(east, shape))

    own = [pair(own_west, own_east, k) for k in range(nz + 1)]
    ghost = [pair(from_west, from_east, k) for k in range(nz + 1)]
    own_kmt, ghost_kmt = own.pop(), ghost.pop()
    outward = jnp.where(left, -1.0, 1.0)
    own_wm = [as_mask(own_kmt > k + 1) for k in range(nz - 1)]
    ghost_wm = [as_mask(ghost_kmt > k + 1) for k in range(nz - 1)]
    side_mask = [as_mask(jnp.minimum(own_kmt, ghost_kmt) > k) for k in range(nz)]

    def side_density(values):
        return [density_of(v, pltpu.roll(v, cols - 1, 1)) for v in values]

    own_density, ghost_density = side_density(own), side_density(ghost)
    own_strat = level_lists(own_density, own_wm)[1]
    ghost_strat = level_lists(ghost_density, ghost_wm)[1]
    side_slope = []
    for k in range(nz):
        s = outward * slope_at(ghost_density[k], own_density[k], side_mask[k], 0.5 * own_strat[k], 0.5 * ghost_strat[k])
        side_slope.append(both(s[:, :1], s[:, half : half + 1]))

    flat = (nz, cols)
    depth = rows_of(flat)

    def ends(index):
        first, second = even_ref[pl.ds(index, nz), :], odd_ref[pl.ds(index, nz), :]
        return jnp.where(odd, first, second), jnp.where(odd, second, first)

    def own_rows(t):
        start = t * nz * rows
        return x_ref[pl.ds(start, nz, stride=rows), :], x_ref[pl.ds(start + rows - 1, nz, stride=rows), :]

    south_kmt, north_kmt = ends(nt * nz)
    south_kmt = jnp.where(bottom, 0.0, south_kmt)
    low_kmt, high_kmt = jnp.broadcast_to(kmt[:1], flat), jnp.broadcast_to(kmt[rows - 1 :], flat)
    level = depth.astype(jnp.float32)

    def end_slope(kmts, heats, salts):
        masks = [as_mask(k > level + 1.0) for k in kmts]
        mask = as_mask(jnp.minimum(*kmts) > level)
        densities = [density_of(h, s) for h, s in zip(heats, salts)]
        strats = [0.5 * level_rows(d, m)[1] for d, m in zip(densities, masks)]
        return masks, mask, slope_at(densities[1], densities[0], mask, *strats)

    heat_ends, salt_ends, heat_own, salt_own = ends(0), ends(nz), own_rows(0), own_rows(1)
    south_wms, south_mask, south_slope = end_slope((south_kmt, low_kmt), (heat_ends[0], heat_own[0]), (salt_ends[0], salt_own[0]))
    north_wms, north_mask, north_slope = end_slope((high_kmt, north_kmt), (heat_own[1], heat_ends[1]), (salt_own[1], salt_ends[1]))

    heat = [x_ref[pl.ds(k * rows, rows), :] for k in range(nz)]
    salt = [x_ref[pl.ds((nz + k) * rows, rows), :] for k in range(nz)]
    density = [density_of(h, s) for h, s in zip(heat, salt)]
    wm = [as_mask(kmt > k + 1) for k in range(nz - 1)]
    strat = [0.5 * s for s in level_lists(density, wm)[1]]
    kmt_x = jnp.minimum(kmt, pltpu.roll(kmt, 1, 1))
    kmt_y = jnp.minimum(kmt, pltpu.roll(kmt, 1, 0))
    sum_x, sum_y = [], []
    for k in range(nz):
        part = pl.ds(k * rows, rows)
        mask = as_mask(kmt_x > k)
        slope = slope_at(density[k], pltpu.roll(density[k], 1, 1), mask, strat[k], pltpu.roll(strat[k], 1, 1))
        ax_ref[part, :] = jnp.where(lane == 0, 0.0, REDI * mask)
        bx_ref[part, :] = jnp.where(lane == 0, 0.0, FACE * slope)
        slope = jnp.where(lane == 0, side_slope[k], slope)
        sum_x.append(slope + jnp.where(lane == cols - 1, side_slope[k], pltpu.roll(slope, cols - 1, 1)))
        mask = as_mask(kmt_y > k)
        slope = slope_at(density[k], pltpu.roll(density[k], 1, 0), mask, strat[k], pltpu.roll(strat[k], 1, 0))
        ay_ref[part, :] = jnp.where(row == 0, 0.0, REDI * mask)
        by_ref[part, :] = jnp.where(row == 0, 0.0, FACE * slope)
        slope = jnp.where(row == 0, jnp.broadcast_to(south_slope[k : k + 1], shape), slope)
        sum_y.append(slope + jnp.where(row == rows - 1, jnp.broadcast_to(north_slope[k : k + 1], shape), pltpu.roll(slope, rows - 1, 0)))
    side_p = []
    for k in range(nz - 1):
        part = pl.ds(k * rows, rows)
        level_x = 0.25 * (sum_x[k] + sum_x[k + 1])
        level_y = 0.25 * (sum_y[k] + sum_y[k + 1])
        p = LEVEL * level_x * wm[k]
        wm_ref[part, :] = wm[k]
        p_ref[part, :] = p
        q_ref[part, :] = LEVEL * level_y * wm[k]
        z_ref[part, :] = REDI * (level_x * level_x + level_y * level_y) * wm[k]
        side_p.append(both(p[:, :1], p[:, cols - 1 :]))
    q_ref[pl.ds((nz - 1) * rows, rows), :] = jnp.zeros(shape, jnp.float32)

    own_sum, ghost_sum = level_lists(own, own_wm)[1], level_lists(ghost, ghost_wm)[1]
    grad = [REDI * side_mask[k] * (ghost[k] - own[k]) for k in range(nz)]
    flux = [grad[k] + outward * FACE * side_slope[k] * (own_sum[k] + ghost_sum[k]) for k in range(nz)]
    tilt = [side_p[k] * outward * (grad[k] + grad[k + 1]) for k in range(nz - 1)]
    turn = lax.rem(lane + 1, cols)
    index = jnp.where(lax.rem(lane, 2) == 0, lane // 2, half + turn // 2)
    for k in range(nz):
        added = flux[k]
        if k < nz - 1:
            added = added + tilt[k]
        if k > 0:
            added = added - tilt[k - 1]
        side_ref[pl.ds(k * rows, rows), :] = jnp.take_along_axis(added, index, axis=1, mode="promise_in_bounds")

    end_coefs = []
    for wms, mask, slope, first in ((south_wms, south_mask, south_slope, 0), (north_wms, north_mask, north_slope, rows - 1)):
        end_coefs.append((wms, REDI * mask, FACE * slope, q_ref[pl.ds(first, nz, stride=rows), :]))
    outer = (lane == 0) | (lane == cols - 1)

    def cell_step(t, carry):
        def load(ref, k):
            return ref[pl.ds(k * rows, rows), :]

        base = t * (nz * rows)
        value = [x_ref[pl.ds(pl.multiple_of(base + k * rows, rows), rows), :] for k in range(nz)]
        diff, total = level_lists(value, [load(wm_ref, k) for k in range(nz - 1)])
        shift = lax.rem(cols - 2 * t, cols)
        new, cell_x, cell_y = [], [], []
        for k in range(nz):
            grad = load(ax_ref, k) * (value[k] - pltpu.roll(value[k], 1, 1))
            flux = grad + load(bx_ref, k) * (total[k] + pltpu.roll(total[k], 1, 1))
            cell_x.append(grad + pltpu.roll(grad, cols - 1, 1))
            gain = pltpu.roll(flux, cols - 1, 1) - flux
            grad = load(ay_ref, k) * (value[k] - pltpu.roll(value[k], 1, 0))
            flux = grad + load(by_ref, k) * (total[k] + pltpu.roll(total[k], 1, 0))
            cell_y.append(grad + pltpu.roll(grad, rows - 1, 0))
            gain = gain + (pltpu.roll(flux, rows - 1, 0) - flux)
            gain = gain + jnp.where(outer, pltpu.roll(load(side_ref, k), shift, 1), 0.0)
            new.append(value[k] + gain)
        down = None
        for k in range(nz):
            result = new[k]
            if k > 0:
                result = result - down
            if k < nz - 1:
                down = (load(p_ref, k) * (cell_x[k] + cell_x[k + 1]) + load(q_ref, k) * (cell_y[k] + cell_y[k + 1])
                        + load(z_ref, k) * diff[k])
                result = result + down
            out_ref[pl.ds(pl.multiple_of(base + k * rows, rows), rows), :] = result
        return carry

    def end_step(t):
        for end in (0, 1):
            wms, a, b, q = end_coefs[end]
            here, there = own_rows(t)[end], ends(t * nz)[end]
            below, above = (there, here) if end == 0 else (here, there)
            sums = level_rows(below, wms[0])[1] + level_rows(above, wms[1])[1]
            grad = a * (above - below)
            flux = grad + b * sums
            tilt = q * (grad + pltpu.roll(grad, nz - 1, 0))
            gain = flux if end == 1 else -flux
            part = pl.ds(t * nz * rows + (rows - 1 if end else 0), nz, stride=rows)
            out_ref[part, :] = out_ref[part, :] + (gain + (tilt - pltpu.roll(tilt, 1, 0)))

    step = nt // CHUNKS
    copies = []
    for c in range(CHUNKS):
        lax.fori_loop(c * step, (c + 1) * step, cell_step, 0)
        for t in range(c * step, (c + 1) * step):
            end_step(t)
        part = pl.ds(c * step * nz * rows, step * nz * rows)
        copies.append(pltpu.make_async_copy(out_ref.at[part], out_hbm.at[part], sems.at[c]))
        copies[-1].start()
    for copy in copies:
        copy.wait()


def row_pairs(color, lons, lats):
    pairs = []
    for lon in range(lons):
        for lat in range(lats - 1):
            if lat % 2 == color:
                pairs += [(lon * lats + lat, lon * lats + lat + 1), (lon * lats + lat + 1, lon * lats + lat)]
        if (lats - 1) % 2 == color:
            pairs.append((lon * lats + lats - 1, (lons - 1 - lon) * lats + lats - 1))
    free_in = sorted(set(range(lons * lats)) - {b for _, b in pairs})
    free_out = set(range(lons * lats)) - {a for a, _ in pairs}
    for target in free_in:
        lon, lat = divmod(target, lats)
        source = (lon ^ 1 if lons % 2 == 0 else (lon + 1) % lons) * lats + lat
        assert source in free_out
        pairs.append((source, target))
    return pairs


def local(tracers, kmt):
    nt, nz, rows, cols = tracers.shape
    lons, lats = lax.axis_size("lon"), lax.axis_size("lat")
    dims = (nt, nz, rows, cols, (lats - 1) % 2)
    per = cols // nt
    packed = ((nz // per + 1) * rows, cols)
    edge = (nt * nz + nz, cols)
    lat = lax.axis_index("lat")
    info = jnp.stack([lat % 2, (lat == lats - 1).astype(jnp.int32), (lat == 0).astype(jnp.int32)])
    vmem = pl.BlockSpec(memory_space=pltpu.VMEM)
    smem = pl.BlockSpec(memory_space=pltpu.SMEM)
    anywhere = pl.BlockSpec(memory_space=pl.ANY)
    x = tracers.reshape(nt * nz * rows, cols)
    x_near, east, west, even, odd = pl.pallas_call(
        functools.partial(pack_kernel, dims),
        out_shape=[pltpu.VMEM(s, jnp.float32) for s in (x.shape, packed, packed, edge, edge)],
        in_specs=[smem, anywhere, vmem],
        out_specs=[vmem] * 5,
        scratch_shapes=[pltpu.SemaphoreType.DMA((CHUNKS,))],
        name="pack",
    )(info, x, kmt)
    ring = [(i, (i + 1) % lons) for i in range(lons)]
    from_west = lax.ppermute(east, "lon", ring)
    from_odd = lax.ppermute(odd, ("lon", "lat"), row_pairs(1, lons, lats))
    from_even = lax.ppermute(even, ("lon", "lat"), row_pairs(0, lons, lats))
    from_east = lax.ppermute(west, "lon", [(b, a) for a, b in ring])
    cells = lambda levels: pltpu.VMEM((levels * rows, cols), jnp.float32)
    out = pl.pallas_call(
        functools.partial(main_kernel, dims),
        out_shape=jax.ShapeDtypeStruct(x.shape, jnp.float32),
        in_specs=[smem] + [vmem] * 8,
        out_specs=anywhere,
        scratch_shapes=[pltpu.VMEM(x.shape, jnp.float32)] + [cells(nz)] * 4 + [cells(nz - 1)] * 2 + [cells(nz), cells(nz - 1), cells(nz)]
        + [pltpu.SemaphoreType.DMA((CHUNKS,))],
        name="step",
    )(info, x_near, kmt, east, west, from_west, from_east, from_even, from_odd)
    return out.reshape(tracers.shape)


def solution(mesh):
    return jax.shard_map(
        local,
        mesh=mesh,
        in_specs=(P(None, None, "lat", "lon"), P("lat", "lon")),
        out_specs=P(None, None, "lat", "lon"),
        check_vma=False,
    )
```

time: 58.6 us -> 25.4 us (0.43)
  the two profiles are of different devices: /device:TPU:0 before, /device:TPU:5 now
where the time goes in v1:
time: 25.4 us; the launch traced here: 25.2 us
  Pallas kernels  12.6 us (50%)
  starting transfers between devices  9.09 us (36%)
  local copies, waits for them, and re-layouts  1.78 us (7%)
  waiting for transfers between devices  1.09 us (4%)
  other arithmetic  0.59 us (2%)
    pallas_call x1, Pallas kernels, local(): pl.pallas_call(functools.partial(main_kernel, dims), out_shape=jax.ShapeD...  9.81 us
    ppermute x1, starting transfers between devices, local(): from_odd = lax.ppermute(odd, ('lon', 'lat'), row_pairs(1, lons, lats))  4.25 us
    ppermute x1, starting transfers between devices, local(): from_east = lax.ppermute(west, 'lon', [(b, a) for a, b in ring])  3.91 us
    pallas_call x1, Pallas kernels, local(): pl.pallas_call(functools.partial(pack_kernel, dims), out_shape=[pltpu.VME...  2.75 us
    unnamed x14, local copies, waits for them, and re-layouts  1.78 us
    ppermute x1, waiting for transfers between devices, local(): from_west = lax.ppermute(east, 'lon', ring)  1.08 us
    ppermute x1, starting transfers between devices, local(): from_even = lax.ppermute(even, ('lon', 'lat'), row_pairs(0, lons, lats))  0.68 us
    another operation x1, other arithmetic, local(): jnp.stack([lat % 2, (lat == lats - 1).astype(jnp.int32), (lat == 0).astyp...  0.59 us
  transfers between devices with their start and end apart: 4, of which 1 were waited for; matrix products, arithmetic and copies ran while one was open for 0% of the time, Pallas kernels for 0%

profile of v1, /device:TPU:5, one launch (start us, length us, event | category | flops | bytes accessed | tf_op | source)
XLA Modules:
  0.0 25.2 jit_solution(9432390145333024639)
XLA Ops:
  0.0 0.6 %pad_add_fusion.info = s32[3]{0:T(128)} fusion(s32[1]{0:T(128)} %bitcast.2, s32[1]{0:T(128)} %bitcast.1, s32[1]{0:T(128)} %bitcast), kind=kLoop, calls=%fused_computation | loop fusion | flops 6 | bytes 24 | tf_op jit(solution)/shard_map/stack | solution.py:307
  0.6 2.7 %pack.1 = (f32[2560,128]{1,0:T(8,128)S(1)}, f32[24,128]{1,0:T(8,128)S(1)}, f32[24,128]{1,0:T(8,128)S(1)}, f32[328,128]{1,0:T(8,128)S(1)}, f32[328,128]{1,0:T(8,128)S(1)}) custom-call(s32[3]{0:T(128)} %pad_add_fusion.info, f32[2560,128]{1,0:T(8,128)} %bitcast.5, s32[8,128]{1,0:T(8,128)} %kmt_ref.3), custom_call_target="tpu_custom_call" | custom-call | tf_op jit(solution)/shard_map/pack/pallas_call | solution.py:312
  3.3 0.0 copy-start
  3.4 1.1 %copy-done = f32[2560,128]{1,0:T(8,128)} copy-done((f32[2560,128]{1,0:T(8,128)}, f32[2560,128]{1,0:T(8,128)S(1)}, u32[]{:S(2)}) %copy-start) | copy-done | bytes 1310744
  4.4 0.0 copy-start.1
  4.4 0.0 copy-start.2
  4.4 0.7 %collective-permute-start.2 = (f32[328,128]{1,0:T(8,128)S(1)}, f32[328,128]{1,0:T(8,128)S(1)}, u32[]{:S(2)}, u32[]{:S(2)}) collective-permute-start(f32[328,128]{1,0:T(8,128)S(1)} %get-tuple-element.13), channel_id=1, source_target_pairs={{0,1},{1,0},{2,3},{3,2},{4,5},{5,4},{6,7},{7,6},{8,9},{9,8},{10,11... | collective-permute-start | bytes 503816 | tf_op jit(solution)/shard_map/ppermute | solution.py:323
  5.1 4.2 %collective-permute-start.3 = (f32[328,128]{1,0:T(8,128)S(1)}, f32[328,128]{1,0:T(8,128)S(1)}, u32[]{:S(2)}, u32[]{:S(2)}) collective-permute-start(f32[328,128]{1,0:T(8,128)S(1)} %get-tuple-element.14), channel_id=1, source_target_pairs={{1,2},{2,1},{3,31},{5,6},{6,5},{7,27},{9,10},{10,9},{11,23},{13,14... | collective-permute-start | bytes 503816 | tf_op jit(solution)/shard_map/ppermute | solution.py:322
  9.4 0.3 %collective-permute-start = (f32[24,128]{1,0:T(8,128)S(1)}, f32[24,128]{1,0:T(8,128)S(1)}, u32[]{:S(2)}, u32[]{:S(2)}) collective-permute-start(f32[24,128]{1,0:T(8,128)S(1)} %get-tuple-element.11.own_east), channel_id=1, source_target_pairs={{0,4},{4,8},{8,12},{12,16},{16,20},{20,24},{24,28},{28,0},{1,5},{5... | collective-permute-start | bytes 36872 | tf_op jit(solution)/shard_map/ppermute | solution.py:321
  9.6 3.9 %collective-permute-start.1 = (f32[24,128]{1,0:T(8,128)S(1)}, f32[24,128]{1,0:T(8,128)S(1)}, u32[]{:S(2)}, u32[]{:S(2)}) collective-permute-start(f32[24,128]{1,0:T(8,128)S(1)} %get-tuple-element.12.own_west), channel_id=1, source_target_pairs={{4,0},{8,4},{12,8},{16,12},{20,16},{24,20},{28,24},{0,28},{5,1},{9... | collective-permute-start | bytes 36872 | tf_op jit(solution)/shard_map/ppermute | solution.py:324
  13.5 1.1 %collective-permute-done.from_west = f32[24,128]{1,0:T(8,128)S(1)} collective-permute-done((f32[24,128]{1,0:T(8,128)S(1)}, f32[24,128]{1,0:T(8,128)S(1)}, u32[]{:S(2)}, u32[]{:S(2)}) %collective-permute-start) | collective-permute-done | bytes 12320 | tf_op jit(solution)/shard_map/ppermute | solution.py:321
  14.6 0.0 copy-start.5
  14.6 0.0 collective-permute-done.1.from_east
  14.6 0.0 collective-permute-done.2.even_ref
  14.6 0.0 copy-start.3
  14.6 0.0 collective-permute-done.3.odd_ref
  14.6 0.0 copy-start.4
  14.7 0.0 copy-done.1
  14.7 0.0 copy-done.2
  14.7 0.5 %copy-done.5 = f32[24,128]{1,0:T(8,128)} copy-done((f32[24,128]{1,0:T(8,128)}, f32[24,128]{1,0:T(8,128)S(1)}, u32[]{:S(2)}) %copy-start.5) | copy-done | bytes 12312
  15.2 0.0 copy-done.6
  15.2 0.1 copy-done.3
  15.3 0.1 copy-done.4
  15.4 9.8 %step.1 = f32[2560,128]{1,0:T(8,128)} custom-call(s32[3]{0:T(128)} %pad_add_fusion.info, f32[2560,128]{1,0:T(8,128)} %copy-done, s32[8,128]{1,0:T(8,128)} %kmt_ref.3, f32[24,128]{1,0:T(8,128)} %copy-done.1, f32[24,128]{1,0:T(8,128)} %copy-done.2, f32[24,128]{1,0:T(8,128)} %copy-done.5, f32[24,128]{1,0:T(8,128)} %copy-done.6, f32[328,128]{1,0:T(8,128)} %copy-done.3, ...), custom_call_target="tpu_custom_call" | custom-call | tf_op jit(solution)/shard_map/step/pallas_call | solution.py:326
  (1 shorter events, 0.0 us)
Async XLA Ops:
  3.3 1.1 %copy-start = (f32[2560,128]{1,0:T(8,128)}, f32[2560,128]{1,0:T(8,128)S(1)}, u32[]{:S(2)}) copy-start(f32[2560,128]{1,0:T(8,128)S(1)} %get-tuple-element.10.x_ref) | copy-start | bytes 3932164
  4.4 10.2 %copy-start.1 = (f32[24,128]{1,0:T(8,128)}, f32[24,128]{1,0:T(8,128)S(1)}, u32[]{:S(2)}) copy-start(f32[24,128]{1,0:T(8,128)S(1)} %get-tuple-element.11.own_east) | copy-start | bytes 36868
  4.4 10.2 %copy-start.2 = (f32[24,128]{1,0:T(8,128)}, f32[24,128]{1,0:T(8,128)S(1)}, u32[]{:S(2)}) copy-start(f32[24,128]{1,0:T(8,128)S(1)} %get-tuple-element.12.own_west) | copy-start | bytes 36868
  4.4 10.2 %collective-permute-start.2 = (f32[328,128]{1,0:T(8,128)S(1)}, f32[328,128]{1,0:T(8,128)S(1)}, u32[]{:S(2)}, u32[]{:S(2)}) collective-permute-start(f32[328,128]{1,0:T(8,128)S(1)} %get-tuple-element.13), channel_id=1, source_target_pairs={{0,1},{1,0},{2,3},{3,2},{4,5},{5,4},{6,7},{7,6},{8,9},{9,8},{10,11... | collective-permute-start | bytes 503816 | tf_op jit(solution)/shard_map/ppermute | solution.py:323
  5.1 9.5 %collective-permute-start.3 = (f32[328,128]{1,0:T(8,128)S(1)}, f32[328,128]{1,0:T(8,128)S(1)}, u32[]{:S(2)}, u32[]{:S(2)}) collective-permute-start(f32[328,128]{1,0:T(8,128)S(1)} %get-tuple-element.14), channel_id=1, source_target_pairs={{1,2},{2,1},{3,31},{5,6},{6,5},{7,27},{9,10},{10,9},{11,23},{13,14... | collective-permute-start | bytes 503816 | tf_op jit(solution)/shard_map/ppermute | solution.py:322
  9.4 5.2 %collective-permute-start = (f32[24,128]{1,0:T(8,128)S(1)}, f32[24,128]{1,0:T(8,128)S(1)}, u32[]{:S(2)}, u32[]{:S(2)}) collective-permute-start(f32[24,128]{1,0:T(8,128)S(1)} %get-tuple-element.11.own_east), channel_id=1, source_target_pairs={{0,4},{4,8},{8,12},{12,16},{16,20},{20,24},{24,28},{28,0},{1,5},{5... | collective-permute-start | bytes 36872 | tf_op jit(solution)/shard_map/ppermute | solution.py:321
  9.6 5.0 %collective-permute-start.1 = (f32[24,128]{1,0:T(8,128)S(1)}, f32[24,128]{1,0:T(8,128)S(1)}, u32[]{:S(2)}, u32[]{:S(2)}) collective-permute-start(f32[24,128]{1,0:T(8,128)S(1)} %get-tuple-element.12.own_west), channel_id=1, source_target_pairs={{4,0},{8,4},{12,8},{16,12},{20,16},{24,20},{28,24},{0,28},{5,1},{9... | collective-permute-start | bytes 36872 | tf_op jit(solution)/shard_map/ppermute | solution.py:324
  14.6 0.6 %copy-start.5 = (f32[24,128]{1,0:T(8,128)}, f32[24,128]{1,0:T(8,128)S(1)}, u32[]{:S(2)}) copy-start(f32[24,128]{1,0:T(8,128)S(1)} %collective-permute-done.from_west) | copy-start | bytes 36868
  14.6 0.6 %copy-start.6 = (f32[24,128]{1,0:T(8,128)}, f32[24,128]{1,0:T(8,128)S(1)}, u32[]{:S(2)}) copy-start(f32[24,128]{1,0:T(8,128)S(1)} %collective-permute-done.1.from_east) | copy-start | bytes 36868
  14.6 0.7 %copy-start.3 = (f32[328,128]{1,0:T(8,128)}, f32[328,128]{1,0:T(8,128)S(1)}, u32[]{:S(2)}) copy-start(f32[328,128]{1,0:T(8,128)S(1)} %collective-permute-done.2.even_ref) | copy-start | bytes 503812
  14.6 0.7 %copy-start.4 = (f32[328,128]{1,0:T(8,128)}, f32[328,128]{1,0:T(8,128)S(1)}, u32[]{:S(2)}) copy-start(f32[328,128]{1,0:T(8,128)S(1)} %collective-permute-done.3.odd_ref) | copy-start | bytes 503812

commit v2 on v1

v2 whole, which is shorter than its diff:
```python
import functools

import jax
import jax.numpy as jnp
from jax import lax
from jax.experimental import pallas as pl
from jax.experimental.pallas import tpu as pltpu
from jax.sharding import PartitionSpec as P

THERMAL = 0.2
HALINE = 0.8
REDI = 0.1
SKEW = 0.05
SLOPE_MAX = 0.6
SLOPE_WIDTH = 0.2
FACE = 0.25 * (REDI - SKEW)
LEVEL = 0.25 * (REDI + SKEW) / REDI
CHUNKS = 5
UNROLL = 8


def taper(slope):
    return slope * 0.5 * (1.0 + jnp.tanh((SLOPE_MAX - jnp.abs(slope)) * (1.0 / SLOPE_WIDTH)))


def lanes_of(shape):
    return lax.broadcasted_iota(jnp.int32, shape, len(shape) - 1)


def rows_of(shape):
    return lax.broadcasted_iota(jnp.int32, shape, len(shape) - 2)


def density_of(heat, salt):
    return HALINE * salt - THERMAL * heat


def as_mask(flag):
    return jnp.where(flag, 1.0, 0.0)


def slope_at(here, there, mask, strat_here, strat_there):
    return taper((here - there) * mask / jnp.maximum(0.5 * (strat_here + strat_there), 1.0))


def level_lists(values, masks):
    diffs = [(values[k + 1] - values[k]) * masks[k] for k in range(len(values) - 1)]
    sums = [diffs[0]] + [a + b for a, b in zip(diffs, diffs[1:])] + [diffs[-1]]
    return diffs, sums


def level_rows(values, mask):
    diffs = (pltpu.roll(values, values.shape[0] - 1, 0) - values) * mask
    return diffs, diffs + pltpu.roll(diffs, 1, 0)


def position():
    lat = lax.axis_index("lat")
    return lax.rem(lat, 2) == 1, lat == 0, lat == lax.axis_size("lat") - 1


def pick(values, index):
    return jnp.take_along_axis(values, index, axis=1, mode="promise_in_bounds")


def pair_of(west, east, cols=128):
    shape = (west.shape[0], cols)
    return jnp.where(lax.rem(lanes_of(shape), 2) == 0, jnp.broadcast_to(west, shape), jnp.broadcast_to(east, shape))


def pack_kernel(dims, x_hbm, kmt_hbm, x_ref, own_ref, east_ref, west_ref, even_ref, odd_ref, kmt_ref, raw_ref, sems):
    nt, nz, rows, cols, mirror_color = dims
    per = cols // nt
    step = nt // CHUNKS
    copies = []
    for c in range(CHUNKS):
        part = pl.ds(c * step * nz * rows, step * nz * rows)
        copies.append(pltpu.make_async_copy(x_hbm.at[part], x_ref.at[part], sems.at[c]))
        copies[-1].start()
    kmt_copy = pltpu.make_async_copy(kmt_hbm, raw_ref, sems.at[CHUNKS])
    kmt_copy.start()
    shape = (rows, cols)
    lane = lanes_of(shape)
    odd, _, top = position()

    def put_rows(low, high, start):
        index = lanes_of(low.shape)
        turned = pick(high, jnp.where(top, cols - 1 - index, index))
        for color, ref in ((0, even_ref), (1, odd_ref)):
            up = turned if color == mirror_color else high
            goes_up = odd if color == 1 else jnp.logical_not(odd)
            ref[pl.ds(start, nz), :] = jnp.where(goes_up, up, low)

    pairs = [jnp.zeros(shape, jnp.float32)] * nz
    for c in range(CHUNKS):
        copies[c].wait()
        for t in range(c * step, (c + 1) * step):
            here = (lane == 2 * t) | (lane == (2 * t - 1) % cols)
            for k in range(nz):
                value = x_ref[pl.ds((t * nz + k) * rows, rows), :]
                pairs[k] = jnp.where(here, pltpu.roll(value, 2 * t, 1) if t else value, pairs[k])
    kmt_copy.wait()
    kmt = raw_ref[...].astype(jnp.float32)
    kmt_ref[...] = kmt
    for k in range(nz):
        own_ref[pl.ds(k * rows, rows), :] = pairs[k]
    for j in range(nz // per + 1):
        east = west = jnp.zeros(shape, jnp.float32)
        for i in range(per):
            k, start = j * per + i, i * nt
            if k > nz:
                break
            index = lax.rem(2 * (lane - start + cols), cols)
            if k == nz:
                side = (jnp.broadcast_to(kmt[:, cols - 1 :], shape), jnp.broadcast_to(kmt[:, :1], shape))
            else:
                side = pick(pairs[k], lax.rem(index + cols - 1, cols)), pick(pairs[k], index)
            east, west = (jnp.where(lane >= start, a, b) for a, b in zip(side, (east, west)))
        east_ref[pl.ds(j * rows, rows), :] = east
        west_ref[pl.ds(j * rows, rows), :] = west
    for t in range(nt):
        start = t * nz * rows
        put_rows(x_ref[pl.ds(start, nz, stride=rows), :], x_ref[pl.ds(start + rows - 1, nz, stride=rows), :], t * nz)
    put_rows(jnp.broadcast_to(kmt[:1], (nz, cols)), jnp.broadcast_to(kmt[rows - 1 :], (nz, cols)), nt * nz)


def inner_kernel(dims, x_ref, kmt_ref, base_ref, cx_ref, cy_ref, diff_ref, sum_x_ref, sum_y_ref, inner_ref,
                 ax_ref, bx_ref, ay_ref, by_ref):
    nt, nz, rows, cols, _ = dims
    shape = (rows, cols)
    lane, row = lanes_of(shape), rows_of(shape)
    kmt = kmt_ref[...]
    heat = [x_ref[pl.ds(k * rows, rows), :] for k in range(nz)]
    salt = [x_ref[pl.ds((nz + k) * rows, rows), :] for k in range(nz)]
    density = [density_of(h, s) for h, s in zip(heat, salt)]
    wm = [as_mask(kmt > k + 1) for k in range(nz - 1)]
    kmt_w = pltpu.roll(kmt, 1, 1)
    wm_w = [as_mask(kmt_w > k + 1) for k in range(nz - 1)]
    strat = [0.5 * s for s in level_lists(density, wm)[1]]
    kmt_x = jnp.where(lane == 0, 0.0, jnp.minimum(kmt, kmt_w))
    kmt_y = jnp.where(row == 0, 0.0, jnp.minimum(kmt, pltpu.roll(kmt, 1, 0)))
    for k in range(nz):
        part = pl.ds(k * rows, rows)
        mask = as_mask(kmt_x > k)
        slope = slope_at(density[k], pltpu.roll(density[k], 1, 1), mask, strat[k], pltpu.roll(strat[k], 1, 1))
        ax_ref[part, :] = REDI * mask
        bx_ref[part, :] = FACE * slope
        sum_x_ref[part, :] = slope + pltpu.roll(slope, cols - 1, 1)
        inner_ref[part, :] = pair_of(slope[:, 1:2], slope[:, cols - 1 :])
        mask = as_mask(kmt_y > k)
        slope = slope_at(density[k], pltpu.roll(density[k], 1, 0), mask, strat[k], pltpu.roll(strat[k], 1, 0))
        ay_ref[part, :] = REDI * mask
        by_ref[part, :] = FACE * slope
        sum_y_ref[part, :] = slope + pltpu.roll(slope, rows - 1, 0)

    def load(ref, k):
        return ref[pl.ds(k * rows, rows), :]

    def tracer(t):
        base = t * (nz * rows)
        part = lambda k: pl.ds(pl.multiple_of(base + k * rows, rows), rows)
        value = [x_ref[part(k), :] for k in range(nz)]
        beside = [pltpu.roll(v, 1, 1) for v in value]
        diff, total = level_lists(value, wm)
        total_w = level_lists(beside, wm_w)[1]
        cell_x, cell_y = [], []
        for k in range(nz):
            grad = load(ax_ref, k) * (value[k] - beside[k])
            flux = grad + load(bx_ref, k) * (total[k] + total_w[k])
            cell_x.append(grad + pltpu.roll(grad, cols - 1, 1))
            gain = pltpu.roll(flux, cols - 1, 1) - flux
            grad = load(ay_ref, k) * (value[k] - pltpu.roll(value[k], 1, 0))
            flux = grad + load(by_ref, k) * (total[k] + pltpu.roll(total[k], 1, 0))
            cell_y.append(grad + pltpu.roll(grad, rows - 1, 0))
            base_ref[part(k), :] = value[k] + (gain + (pltpu.roll(flux, rows - 1, 0) - flux))
        for k in range(nz - 1):
            cx_ref[part(k), :] = cell_x[k] + cell_x[k + 1]
            cy_ref[part(k), :] = cell_y[k] + cell_y[k + 1]
            diff_ref[part(k), :] = diff[k]

    def block(i, carry):
        for t in range(UNROLL):
            tracer(i * UNROLL + t)
        return carry

    lax.fori_loop(0, nt // UNROLL, block, 0)


def outer_kernel(dims, x_ref, kmt_ref, own_ref, base_ref, cx_ref, cy_ref, diff_ref, sum_x_ref, sum_y_ref, inner_ref,
                 from_west, from_east, even_ref, odd_ref, out_hbm, out_ref, p_ref, q_ref, z_ref, side_ref, sems):
    nt, nz, rows, cols, _ = dims
    per = cols // nt
    shape = (rows, cols)
    lane, row = lanes_of(shape), rows_of(shape)
    odd, bottom, _ = position()
    kmt = kmt_ref[...]

    def load(ref, k):
        return ref[pl.ds(k * rows, rows), :]

    even_lane = lax.rem(lane, 2) == 0
    slot = jnp.where(even_lane, lane // 2, lax.rem(lane + 1, cols) // 2)
    outward = jnp.where(even_lane, -1.0, 1.0)

    def ghost_at(k):
        index = lax.rem(slot + (k % per) * nt, cols)
        return jnp.where(even_lane, pick(load(from_west, k // per), index), pick(load(from_east, k // per), index))

    own = [load(own_ref, k) for k in range(nz)]
    ghost = [ghost_at(k) for k in range(nz + 1)]
    own_kmt, ghost_kmt = pair_of(kmt[:, :1], kmt[:, cols - 1 :]), ghost.pop()
    own_wm = [as_mask(own_kmt > k + 1) for k in range(nz - 1)]
    ghost_wm = [as_mask(ghost_kmt > k + 1) for k in range(nz - 1)]
    side_mask = [as_mask(jnp.minimum(own_kmt, ghost_kmt) > k) for k in range(nz)]

    def side_density(values):
        return [density_of(v, pltpu.roll(v, cols - 2, 1)) for v in values]

    own_density, ghost_density = side_density(own), side_density(ghost)
    own_strat = level_lists(own_density, own_wm)[1]
    ghost_strat = level_lists(ghost_density, ghost_wm)[1]
    first = [
        outward * slope_at(ghost_density[k], own_density[k], side_mask[k], 0.5 * own_strat[k], 0.5 * ghost_strat[k])
        for k in range(nz)
    ]
    side_slope = [pair_of(s[:, :1], s[:, cols - 1 :]) for s in first]
    outer = (lane == 0) | (lane == cols - 1)
    sum_x = [load(sum_x_ref, k) + jnp.where(outer, first[k], 0.0) for k in range(nz)]

    flat = (nz, cols)
    level = rows_of(flat).astype(jnp.float32)

    def ends(index):
        a, b = even_ref[pl.ds(index, nz), :], odd_ref[pl.ds(index, nz), :]
        return jnp.where(odd, a, b), jnp.where(odd, b, a)

    def own_rows(t):
        start = t * nz * rows
        return x_ref[pl.ds(start, nz, stride=rows), :], x_ref[pl.ds(start + rows - 1, nz, stride=rows), :]

    south_kmt, north_kmt = ends(nt * nz)
    south_kmt = jnp.where(bottom, 0.0, south_kmt)
    low_kmt, high_kmt = jnp.broadcast_to(kmt[:1], flat), jnp.broadcast_to(kmt[rows - 1 :], flat)

    def end_slope(kmts, heats, salts):
        masks = [as_mask(k > level + 1.0) for k in kmts]
        mask = as_mask(jnp.minimum(*kmts) > level)
        densities = [density_of(h, s) for h, s in zip(heats, salts)]
        strats = [0.5 * level_rows(d, m)[1] for d, m in zip(densities, masks)]
        return masks, mask, slope_at(densities[1], densities[0], mask, *strats)

    heat_ends, salt_ends, heat_own, salt_own = ends(0), ends(nz), own_rows(0), own_rows(1)
    south = end_slope((south_kmt, low_kmt), (heat_ends[0], heat_own[0]), (salt_ends[0], salt_own[0]))
    north = end_slope((high_kmt, north_kmt), (heat_own[1], heat_ends[1]), (salt_own[1], salt_ends[1]))
    sum_y = []
    for k in range(nz):
        below, above = jnp.broadcast_to(south[2][k : k + 1], shape), jnp.broadcast_to(north[2][k : k + 1], shape)
        sum_y.append(load(sum_y_ref, k) + jnp.where(row == 0, below, jnp.where(row == rows - 1, above, 0.0)))

    for k in range(nz - 1):
        part = pl.ds(k * rows, rows)
        wm = as_mask(kmt > k + 1)
        level_x, level_y = 0.25 * (sum_x[k] + sum_x[k + 1]), 0.25 * (sum_y[k] + sum_y[k + 1])
        p_ref[part, :] = LEVEL * level_x * wm
        q_ref[part, :] = LEVEL * level_y * wm
        z_ref[part, :] = REDI * (level_x * level_x + level_y * level_y) * wm
    q_ref[pl.ds((nz - 1) * rows, rows), :] = jnp.zeros(shape, jnp.float32)

    own_sum, ghost_sum = level_lists(own, own_wm)[1], level_lists(ghost, ghost_wm)[1]
    grad = [REDI * side_mask[k] * (ghost[k] - own[k]) for k in range(nz)]
    flux = [grad[k] + outward * FACE * side_slope[k] * (own_sum[k] + ghost_sum[k]) for k in range(nz)]
    both = [side_slope[k] + load(inner_ref, k) for k in range(nz)]
    tilt = [0.25 * LEVEL * (both[k] + both[k + 1]) * own_wm[k] * outward * (grad[k] + grad[k + 1]) for k in range(nz - 1)]
    for k in range(nz):
        added = flux[k]
        if k < nz - 1:
            added = added + tilt[k]
        if k > 0:
            added = added - tilt[k - 1]
        side_ref[pl.ds(k * rows, rows), :] = added

    end_coefs = []
    for (wms, mask, slope), start in ((south, 0), (north, rows - 1)):
        end_coefs.append((wms, REDI * mask, FACE * slope, q_ref[pl.ds(start, nz, stride=rows), :]))

    def cell_step(t):
        base = t * nz * rows
        part = lambda k: pl.ds(base + k * rows, rows)
        down = None
        for k in range(nz):
            side = load(side_ref, k)
            side = pltpu.roll(side, cols - 2 * t, 1) if t else side
            result = base_ref[part(k), :] + jnp.where(outer, side, 0.0)
            if k > 0:
                result = result - down
            if k < nz - 1:
                down = load(p_ref, k) * cx_ref[part(k), :] + load(q_ref, k) * cy_ref[part(k), :] + load(z_ref, k) * diff_ref[part(k), :]
                result = result + down
            out_ref[part(k), :] = result

    def end_step(t):
        for end in (0, 1):
            wms, a, b, q = end_coefs[end]
            here, there = own_rows(t)[end], ends(t * nz)[end]
            below, above = (there, here) if end == 0 else (here, there)
            sums = level_rows(below, wms[0])[1] + level_rows(above, wms[1])[1]
            grad = a * (above - below)
            flux = grad + b * sums
            tilt = q * (grad + pltpu.roll(grad, nz - 1, 0))
            gain = flux if end == 1 else -flux
            part = pl.ds(t * nz * rows + (rows - 1 if end else 0), nz, stride=rows)
            out_ref[part, :] = out_ref[part, :] + (gain + (tilt - pltpu.roll(tilt, 1, 0)))

    step = nt // CHUNKS
    copies = []
    for c in range(CHUNKS):
        for t in range(c * step, (c + 1) * step):
            cell_step(t)
        for t in range(c * step, (c + 1) * step):
            end_step(t)
        part = pl.ds(c * step * nz * rows, step * nz * rows)
        copies.append(pltpu.make_async_copy(out_ref.at[part], out_hbm.at[part], sems.at[c]))
        copies[-1].start()
    for copy in copies:
        copy.wait()


def row_pairs(color, lons, lats):
    pairs = []
    for lon in range(lons):
        for lat in range(lats - 1):
            if lat % 2 == color:
                pairs += [(lon * lats + lat, lon * lats + lat + 1), (lon * lats + lat + 1, lon * lats + lat)]
        if (lats - 1) % 2 == color:
            pairs.append((lon * lats + lats - 1, (lons - 1 - lon) * lats + lats - 1))
    free_in = sorted(set(range(lons * lats)) - {b for _, b in pairs})
    free_out = set(range(lons * lats)) - {a for a, _ in pairs}
    for target in free_in:
        lon, lat = divmod(target, lats)
        source = (lon ^ 1 if lons % 2 == 0 else (lon + 1) % lons) * lats + lat
        assert source in free_out
        pairs.append((source, target))
    return pairs


def local(tracers, kmt):
    nt, nz, rows, cols = tracers.shape
    lons, lats = lax.axis_size("lon"), lax.axis_size("lat")
    dims = (nt, nz, rows, cols, (lats - 1) % 2)
    packed = ((nz // (cols // nt) + 1) * rows, cols)
    edge = (nt * nz + nz, cols)
    level, block = (nz * rows, cols), (nt * nz * rows, cols)
    vmem, anywhere = pl.BlockSpec(memory_space=pltpu.VMEM), pl.BlockSpec(memory_space=pl.ANY)

    def call(kernel, inputs, out_shape, scratch, flops, specs=None):
        out = [pltpu.VMEM(s, jnp.float32) for s in out_shape] if specs is None else out_shape
        if specs is None:
            specs = [vmem] * len(out_shape)
        near = [a if a is x or a is kmt else pltpu.with_memory_space_constraint(a, pltpu.VMEM) for a in inputs]
        return pl.pallas_call(
            functools.partial(kernel, dims),
            out_shape=out,
            in_specs=[anywhere if a is x or a is kmt else vmem for a in inputs],
            out_specs=specs,
            scratch_shapes=scratch,
            cost_estimate=pl.CostEstimate(flops=flops, bytes_accessed=flops, transcendentals=0),
            compiler_params=pltpu.CompilerParams(vmem_limit_bytes=16 * 2**20),
        )(*near)

    x = tracers.reshape(block)
    cells = lambda levels: pltpu.VMEM((levels * rows, cols), jnp.float32)
    near, own, east, west, even, odd, near_kmt = call(
        pack_kernel,
        (x, kmt),
        (block, level, packed, packed, edge, edge, (rows, cols)),
        [pltpu.VMEM((rows, cols), jnp.int32), pltpu.SemaphoreType.DMA((CHUNKS + 1,))],
        1000000,
    )
    ring = [(i, (i + 1) % lons) for i in range(lons)]
    from_west = lax.ppermute(east, "lon", ring)
    from_odd = lax.ppermute(odd, ("lon", "lat"), row_pairs(1, lons, lats))
    from_even = lax.ppermute(even, ("lon", "lat"), row_pairs(0, lons, lats))
    from_east = lax.ppermute(west, "lon", [(b, a) for a, b in ring])
    inner = call(inner_kernel, (near, near_kmt), (block,) * 4 + (level,) * 3, [cells(nz)] * 4, 10000000)
    out = call(
        outer_kernel,
        (near, near_kmt, own, *inner, from_west, from_east, from_even, from_odd),
        jax.ShapeDtypeStruct(block, jnp.float32),
        [pltpu.VMEM(block, jnp.float32), cells(nz - 1), cells(nz), cells(nz - 1), cells(nz), pltpu.SemaphoreType.DMA((CHUNKS,))],
        10000000,
        anywhere,
    )
    return out.reshape(tracers.shape)


def solution(mesh):
    return jax.shard_map(
        local,
        mesh=mesh,
        in_specs=(P(None, None, "lat", "lon"), P("lat", "lon")),
        out_specs=P(None, None, "lat", "lon"),
        check_vma=False,
    )
```

time: 25.4 us -> 17 us (0.67)
  Pallas kernels: 12.6 us -> 5.56 us
  waiting for transfers between devices: 1.09 us -> 0.01 us
  other arithmetic: 0.59 us -> 0 us
    pallas_call x2 -> x3, Pallas kernels: 12.6 us -> 5.56 us  [call(): pl.pallas_call(functools.partial(kernel, dims), out_shape=out, in_specs=[...]
    ppermute x1, waiting for transfers between devices: 1.08 us -> 0.01 us  [local(): from_west = lax.ppermute(east, 'lon', ring)]
    another operation x1 -> x0, other arithmetic: 0.59 us -> none  [local(): jnp.stack([lat % 2, (lat == lats - 1).astype(jnp.int32), (lat == 0).astyp...]
    unnamed x14 -> x4, local copies, waits for them, and re-layouts: 1.78 us -> 2 us
  transfers between devices with their start and end apart: 4 -> 4, of which waited for: 1 -> 0; matrix products, arithmetic and copies ran while one was open for 0% -> 0% of each run, Pallas kernels for 0% -> 16%
where the time goes in v2:
time: 17 us; the launch traced here: 16.8 us
  starting transfers between devices  9.15 us (54%)
  Pallas kernels  5.56 us (33%)
  local copies, waits for them, and re-layouts  2 us (12%)
    pallas_call x3, Pallas kernels, call(): pl.pallas_call(functools.partial(kernel, dims), out_shape=out, in_specs=[...  5.56 us
    ppermute x1, starting transfers between devices, local(): from_odd = lax.ppermute(odd, ('lon', 'lat'), row_pairs(1, lons, lats))  4.25 us
    ppermute x1, starting transfers between devices, local(): from_east = lax.ppermute(west, 'lon', [(b, a) for a, b in ring])  3.91 us
    unnamed x4, local copies, waits for them, and re-layouts  2 us
    ppermute x1, starting transfers between devices, local(): from_even = lax.ppermute(even, ('lon', 'lat'), row_pairs(0, lons, lats))  0.74 us
  transfers between devices with their start and end apart: 4, of which 0 were waited for; matrix products, arithmetic and copies ran while one was open for 0% of the time, Pallas kernels for 16%

profile of v2, /device:TPU:5, one launch (start us, length us, event | category | flops | bytes accessed | tf_op | source)
XLA Modules:
  0.0 16.8 jit_solution(12361242078752964312)
XLA Ops:
  0.0 0.0 copy-start
  0.0 1.3 %copy-done = f32[40,8,8,128]{3,2,1,0:T(8,128)S(1)} copy-done((f32[40,8,8,128]{3,2,1,0:T(8,128)S(1)}, f32[40,8,8,128]{3,2,1,0:T(8,128)}, u32[]{:S(2)}) %copy-start) | copy-done | bytes 1310744
  1.3 0.0 copy-start.1
  1.3 0.7 %copy-done.1 = s32[8,128]{1,0:T(8,128)S(1)} copy-done((s32[8,128]{1,0:T(8,128)S(1)}, s32[8,128]{1,0:T(8,128)}, u32[]{:S(2)}) %copy-start.1) | copy-done | bytes 4120
  2.0 1.0 %shard_map.28 = (f32[2560,128]{1,0:T(8,128)S(1)}, f32[64,128]{1,0:T(8,128)S(1)}, f32[24,128]{1,0:T(8,128)S(1)}, f32[24,128]{1,0:T(8,128)S(1)}, f32[328,128]{1,0:...) custom-call(f32[2560,128]{1,0:T(8,128)S(1)} %bitcast.2, s32[8,128]{1,0:T(8,128)S(1)} %copy-done.1), custom_call_target="tpu_custom_call" | custom-call | flops 1000000 | bytes 1000000 | tf_op jit(solution)/shard_map/pallas_call | solution.py:360
  3.0 0.7 %collective-permute-start.2 = (f32[328,128]{1,0:T(8,128)S(1)}, f32[328,128]{1,0:T(8,128)S(1)}, u32[]{:S(2)}, u32[]{:S(2)}) collective-permute-start(f32[328,128]{1,0:T(8,128)S(1)} %get-tuple-element.31), channel_id=1, source_target_pairs={{0,1},{1,0},{2,3},{3,2},{4,5},{5,4},{6,7},{7,6},{8,9},{9,8},{10,11... | collective-permute-start | bytes 503816 | tf_op jit(solution)/shard_map/ppermute | solution.py:382
  3.7 4.2 %collective-permute-start.3 = (f32[328,128]{1,0:T(8,128)S(1)}, f32[328,128]{1,0:T(8,128)S(1)}, u32[]{:S(2)}, u32[]{:S(2)}) collective-permute-start(f32[328,128]{1,0:T(8,128)S(1)} %get-tuple-element.32), channel_id=1, source_target_pairs={{1,2},{2,1},{3,31},{5,6},{6,5},{7,27},{9,10},{10,9},{11,23},{13,14... | collective-permute-start | bytes 503816 | tf_op jit(solution)/shard_map/ppermute | solution.py:381
  8.0 0.3 %collective-permute-start = (f32[24,128]{1,0:T(8,128)S(1)}, f32[24,128]{1,0:T(8,128)S(1)}, u32[]{:S(2)}, u32[]{:S(2)}) collective-permute-start(f32[24,128]{1,0:T(8,128)S(1)} %get-tuple-element.29), channel_id=1, source_target_pairs={{0,4},{4,8},{8,12},{12,16},{16,20},{20,24},{24,28},{28,0},{1,5},{5... | collective-permute-start | bytes 36872 | tf_op jit(solution)/shard_map/ppermute | solution.py:380
  8.2 3.9 %collective-permute-start.1 = (f32[24,128]{1,0:T(8,128)S(1)}, f32[24,128]{1,0:T(8,128)S(1)}, u32[]{:S(2)}, u32[]{:S(2)}) collective-permute-start(f32[24,128]{1,0:T(8,128)S(1)} %get-tuple-element.30), channel_id=1, source_target_pairs={{4,0},{8,4},{12,8},{16,12},{20,16},{24,20},{28,24},{0,28},{5,1},{9... | collective-permute-start | bytes 36872 | tf_op jit(solution)/shard_map/ppermute | solution.py:383
  12.1 2.8 %shard_map.29 = (f32[2560,128]{1,0:T(8,128)S(1)}, f32[2560,128]{1,0:T(8,128)S(1)}, f32[2560,128]{1,0:T(8,128)S(1)}, f32[2560,128]{1,0:T(8,128)S(1)}, f32[64,128]...) custom-call(f32[2560,128]{1,0:T(8,128)S(1)} %get-tuple-element.19.x_ref, ...), custom_call_target="tpu_custom_call" | custom-call | flops 10000000 | bytes 10000000 | tf_op jit(solution)/shard_map/pallas_call | solution.py:360
  14.9 0.0 collective-permute-done.from_west
  14.9 0.0 collective-permute-done.1.from_east
  14.9 0.0 collective-permute-done.2.even_ref
  14.9 0.0 collective-permute-done.3.odd_ref
  15.0 1.8 %shard_map.30 = f32[2560,128]{1,0:T(8,128)} custom-call(f32[2560,128]{1,0:T(8,128)S(1)} %get-tuple-element.19.x_ref, f32[8,128]{1,0:T(8,128)S(1)} %get-tuple-element.20.kmt_ref, f32[64,128]{1,0:T(8,128)S(1)} %get-tuple-element.21.own_ref, f32[2560,128]{1,0:T(8,128)S(1)} %get-tuple-element.22.base_ref, f32[2560,128]{1,0:T(8,128)S(1)} %get-tuple-element.23.cx_ref, ...), custom_call_target="tpu_custom_call" | custom-call | flops 10000000 | bytes 10000000 | tf_op jit(solution)/shard_map/pallas_call | solution.py:360
Async XLA Ops:
  0.0 1.3 %copy-start = (f32[40,8,8,128]{3,2,1,0:T(8,128)S(1)}, f32[40,8,8,128]{3,2,1,0:T(8,128)}, u32[]{:S(2)}) copy-start(f32[40,8,8,128]{3,2,1,0:T(8,128)} %param.2) | copy-start | bytes 3932164
  1.3 0.7 %copy-start.1 = (s32[8,128]{1,0:T(8,128)S(1)}, s32[8,128]{1,0:T(8,128)}, u32[]{:S(2)}) copy-start(s32[8,128]{1,0:T(8,128)} %kmt_hbm.1) | copy-start | bytes 12292
  3.0 11.9 %collective-permute-start.2 = (f32[328,128]{1,0:T(8,128)S(1)}, f32[328,128]{1,0:T(8,128)S(1)}, u32[]{:S(2)}, u32[]{:S(2)}) collective-permute-start(f32[328,128]{1,0:T(8,128)S(1)} %get-tuple-element.31), channel_id=1, source_target_pairs={{0,1},{1,0},{2,3},{3,2},{4,5},{5,4},{6,7},{7,6},{8,9},{9,8},{10,11... | collective-permute-start | bytes 503816 | tf_op jit(solution)/shard_map/ppermute | solution.py:382
  3.7 11.2 %collective-permute-start.3 = (f32[328,128]{1,0:T(8,128)S(1)}, f32[328,128]{1,0:T(8,128)S(1)}, u32[]{:S(2)}, u32[]{:S(2)}) collective-permute-start(f32[328,128]{1,0:T(8,128)S(1)} %get-tuple-element.32), channel_id=1, source_target_pairs={{1,2},{2,1},{3,31},{5,6},{6,5},{7,27},{9,10},{10,9},{11,23},{13,14... | collective-permute-start | bytes 503816 | tf_op jit(solution)/shard_map/ppermute | solution.py:381
  8.0 6.9 %collective-permute-start = (f32[24,128]{1,0:T(8,128)S(1)}, f32[24,128]{1,0:T(8,128)S(1)}, u32[]{:S(2)}, u32[]{:S(2)}) collective-permute-start(f32[24,128]{1,0:T(8,128)S(1)} %get-tuple-element.29), channel_id=1, source_target_pairs={{0,4},{4,8},{8,12},{12,16},{16,20},{20,24},{24,28},{28,0},{1,5},{5... | collective-permute-start | bytes 36872 | tf_op jit(solution)/shard_map/ppermute | solution.py:380
  8.2 6.7 %collective-permute-start.1 = (f32[24,128]{1,0:T(8,128)S(1)}, f32[24,128]{1,0:T(8,128)S(1)}, u32[]{:S(2)}, u32[]{:S(2)}) collective-permute-start(f32[24,128]{1,0:T(8,128)S(1)} %get-tuple-element.30), channel_id=1, source_target_pairs={{4,0},{8,4},{12,8},{16,12},{20,16},{24,20},{28,24},{0,28},{5,1},{9... | collective-permute-start | bytes 36872 | tf_op jit(solution)/shard_map/ppermute | solution.py:383

commit v3 on v2

--- a/solution.py
+++ b/solution.py
@@ -16,7 +16,8 @@
 FACE = 0.25 * (REDI - SKEW)
 LEVEL = 0.25 * (REDI + SKEW) / REDI
 CHUNKS = 5
-UNROLL = 8
+UNROLL = 4
+EARLY = 5
 
 
 def taper(slope):
@@ -124,9 +125,31 @@
     put_rows(jnp.broadcast_to(kmt[:1], (nz, cols)), jnp.broadcast_to(kmt[rows - 1 :], (nz, cols)), nt * nz)
 
 
-def inner_kernel(dims, x_ref, kmt_ref, base_ref, cx_ref, cy_ref, diff_ref, sum_x_ref, sum_y_ref, inner_ref,
-                 ax_ref, bx_ref, ay_ref, by_ref):
-    nt, nz, rows, cols, _ = dims
+def starts_early():
+    _, _, top = position()
+    return (lax.axis_index("lon") == 0) & jnp.logical_not(top)
+
+
+def early_kernel(dims, x_ref, kmt_ref, *refs):
+    @pl.when(starts_early())
+    def _():
+        coefs_body(dims, x_ref, kmt_ref, *refs[4:])
+        inner_body(dims, 0, EARLY, x_ref, kmt_ref, *refs)
+
+
+def late_kernel(dims, x_ref, kmt_ref, *refs):
+    refs = refs[len(refs) // 2 :]
+    early = starts_early()
+
+    @pl.when(jnp.logical_not(early))
+    def _():
+        coefs_body(dims, x_ref, kmt_ref, *refs[4:])
+
+    inner_body(dims, jnp.where(early, EARLY, 0), dims[0] // UNROLL, x_ref, kmt_ref, *refs)
+
+
+def coefs_body(dims, x_ref, kmt_ref, sum_x_ref, sum_y_ref, inner_ref, ax_ref, bx_ref, ay_ref, by_ref):
+    _, nz, rows, cols, _ = dims
     shape = (rows, cols)
     lane, row = lanes_of(shape), rows_of(shape)
     kmt = kmt_ref[...]
@@ -135,7 +158,6 @@
     density = [density_of(h, s) for h, s in zip(heat, salt)]
     wm = [as_mask(kmt > k + 1) for k in range(nz - 1)]
     kmt_w = pltpu.roll(kmt, 1, 1)
-    wm_w = [as_mask(kmt_w > k + 1) for k in range(nz - 1)]
     strat = [0.5 * s for s in level_lists(density, wm)[1]]
     kmt_x = jnp.where(lane == 0, 0.0, jnp.minimum(kmt, kmt_w))
     kmt_y = jnp.where(row == 0, 0.0, jnp.minimum(kmt, pltpu.roll(kmt, 1, 0)))
@@ -152,6 +174,15 @@
         ay_ref[part, :] = REDI * mask
         by_ref[part, :] = FACE * slope
         sum_y_ref[part, :] = slope + pltpu.roll(slope, rows - 1, 0)
+
+
+def inner_body(dims, first, last, x_ref, kmt_ref, base_ref, cx_ref, cy_ref, diff_ref, sum_x_ref, sum_y_ref, inner_ref,
+               ax_ref, bx_ref, ay_ref, by_ref):
+    _, nz, rows, cols, _ = dims
+    kmt = kmt_ref[...]
+    kmt_w = pltpu.roll(kmt, 1, 1)
+    wm = [as_mask(kmt > k + 1) for k in range(nz - 1)]
+    wm_w = [as_mask(kmt_w > k + 1) for k in range(nz - 1)]
 
     def load(ref, k):
         return ref[pl.ds(k * rows, rows), :]
@@ -183,7 +214,7 @@
             tracer(i * UNROLL + t)
         return carry
 
-    lax.fori_loop(0, nt // UNROLL, block, 0)
+    lax.fori_loop(first, last, block, 0)
 
 
 def outer_kernel(dims, x_ref, kmt_ref, own_ref, base_ref, cx_ref, cy_ref, diff_ref, sum_x_ref, sum_y_ref, inner_ref,
@@ -352,17 +383,18 @@
     level, block = (nz * rows, cols), (nt * nz * rows, cols)
     vmem, anywhere = pl.BlockSpec(memory_space=pltpu.VMEM), pl.BlockSpec(memory_space=pl.ANY)
 
-    def call(kernel, inputs, out_shape, scratch, flops, specs=None):
+    def call(kernel, inputs, out_shape, scratch, flops, specs=None, aliases={}):
         out = [pltpu.VMEM(s, jnp.float32) for s in out_shape] if specs is None else out_shape
         if specs is None:
             specs = [vmem] * len(out_shape)
-        near = [a if a is x or a is kmt else pltpu.with_memory_space_constraint(a, pltpu.VMEM) for a in inputs]
+        near = [pltpu.with_memory_space_constraint(a, pltpu.HBM if a is x or a is kmt else pltpu.VMEM) for a in inputs]
         return pl.pallas_call(
             functools.partial(kernel, dims),
             out_shape=out,
             in_specs=[anywhere if a is x or a is kmt else vmem for a in inputs],
             out_specs=specs,
             scratch_shapes=scratch,
+            input_output_aliases=aliases,
             cost_estimate=pl.CostEstimate(flops=flops, bytes_accessed=flops, transcendentals=0),
             compiler_params=pltpu.CompilerParams(vmem_limit_bytes=16 * 2**20),
         )(*near)
@@ -378,10 +410,13 @@
     )
     ring = [(i, (i + 1) % lons) for i in range(lons)]
     from_west = lax.ppermute(east, "lon", ring)
+    shapes = (block,) * 4 + (level,) * 7
+    inner = call(early_kernel, (near, near_kmt), shapes, [], 10000000)
     from_odd = lax.ppermute(odd, ("lon", "lat"), row_pairs(1, lons, lats))
     from_even = lax.ppermute(even, ("lon", "lat"), row_pairs(0, lons, lats))
     from_east = lax.ppermute(west, "lon", [(b, a) for a, b in ring])
-    inner = call(inner_kernel, (near, near_kmt), (block,) * 4 + (level,) * 3, [cells(nz)] * 4, 10000000)
+    aliases = {2 + i: i for i in range(len(shapes))}
+    inner = call(late_kernel, (near, near_kmt, *inner), shapes, [], 10000000, aliases=aliases)[:7]
     out = call(
         outer_kernel,
         (near, near_kmt, own, *inner, from_west, from_east, from_even, from_odd),

time: 17 us -> 15.6 us (0.918)
  local copies, waits for them, and re-layouts: 2 us -> 0 us
  Pallas kernels: 5.56 us -> 6.26 us
    unnamed x4 -> x0, local copies, waits for them, and re-layouts: 2 us -> none
    pallas_call x3 -> x4, Pallas kernels: 5.56 us -> 6.26 us  [call(): pl.pallas_call(functools.partial(kernel, dims), out_shape=out, in_specs=[...]
  transfers between devices with their start and end apart: 4 -> 4, of which waited for: 0 -> 0; matrix products, arithmetic and copies ran while one was open for 0% -> 0% of each run, Pallas kernels for 16% -> 17%
where the time goes in v3:
time: 15.6 us; the launch traced here: 15.5 us
  starting transfers between devices  9.15 us (59%)
  Pallas kernels  6.26 us (40%)
    pallas_call x4, Pallas kernels, call(): pl.pallas_call(functools.partial(kernel, dims), out_shape=out, in_specs=[...  6.26 us
    ppermute x1, starting transfers between devices, local(): from_odd = lax.ppermute(odd, ('lon', 'lat'), row_pairs(1, lons, lats))  4.25 us
    ppermute x1, starting transfers between devices, local(): from_east = lax.ppermute(west, 'lon', [(b, a) for a, b in ring])  3.91 us
    ppermute x1, starting transfers between devices, local(): from_even = lax.ppermute(even, ('lon', 'lat'), row_pairs(0, lons, lats))  0.74 us
  transfers between devices with their start and end apart: 4, of which 0 were waited for; matrix products, arithmetic and copies ran while one was open for 0% of the time, Pallas kernels for 17%

profile of v3, /device:TPU:5, one launch (start us, length us, event | category | flops | bytes accessed | tf_op | source)
XLA Modules:
  0.0 15.5 jit_solution(12419221105410467751)
XLA Ops:
  0.0 1.8 %shard_map.28 = (f32[2560,128]{1,0:T(8,128)S(1)}, f32[64,128]{1,0:T(8,128)S(1)}, f32[24,128]{1,0:T(8,128)S(1)}, f32[24,128]{1,0:T(8,128)S(1)}, f32[328,128]{1,0:...) custom-call(f32[2560,128]{1,0:T(8,128)} %bitcast.2, s32[8,128]{1,0:T(8,128)} %kmt_hbm.1), custom_call_target="tpu_custom_call" | custom-call | flops 1000000 | bytes 1000000 | tf_op jit(solution)/shard_map/pallas_call | solution.py:391
  1.8 0.7 %collective-permute-start.2 = (f32[328,128]{1,0:T(8,128)S(1)}, f32[328,128]{1,0:T(8,128)S(1)}, u32[]{:S(2)}, u32[]{:S(2)}) collective-permute-start(f32[328,128]{1,0:T(8,128)S(1)} %get-tuple-element.53), channel_id=1, source_target_pairs={{0,1},{1,0},{2,3},{3,2},{4,5},{5,4},{6,7},{7,6},{8,9},{9,8},{10,11... | collective-permute-start | bytes 503816 | tf_op jit(solution)/shard_map/ppermute | solution.py:416
  2.6 4.2 %collective-permute-start.3 = (f32[328,128]{1,0:T(8,128)S(1)}, f32[328,128]{1,0:T(8,128)S(1)}, u32[]{:S(2)}, u32[]{:S(2)}) collective-permute-start(f32[328,128]{1,0:T(8,128)S(1)} %get-tuple-element.54), channel_id=1, source_target_pairs={{1,2},{2,1},{3,31},{5,6},{6,5},{7,27},{9,10},{10,9},{11,23},{13,14... | collective-permute-start | bytes 503816 | tf_op jit(solution)/shard_map/ppermute | solution.py:415
  6.8 0.3 %collective-permute-start = (f32[24,128]{1,0:T(8,128)S(1)}, f32[24,128]{1,0:T(8,128)S(1)}, u32[]{:S(2)}, u32[]{:S(2)}) collective-permute-start(f32[24,128]{1,0:T(8,128)S(1)} %get-tuple-element.51), channel_id=1, source_target_pairs={{0,4},{4,8},{8,12},{12,16},{16,20},{20,24},{24,28},{28,0},{1,5},{5... | collective-permute-start | bytes 36872 | tf_op jit(solution)/shard_map/ppermute | solution.py:412
  7.1 3.9 %collective-permute-start.1 = (f32[24,128]{1,0:T(8,128)S(1)}, f32[24,128]{1,0:T(8,128)S(1)}, u32[]{:S(2)}, u32[]{:S(2)}) collective-permute-start(f32[24,128]{1,0:T(8,128)S(1)} %get-tuple-element.52), channel_id=1, source_target_pairs={{4,0},{8,4},{12,8},{16,12},{20,16},{24,20},{28,24},{0,28},{5,1},{9... | collective-permute-start | bytes 36872 | tf_op jit(solution)/shard_map/ppermute | solution.py:417
  11.0 2.6 %shard_map.30 = (f32[2560,128]{1,0:T(8,128)S(1)}, f32[2560,128]{1,0:T(8,128)S(1)}, f32[2560,128]{1,0:T(8,128)S(1)}, f32[2560,128]{1,0:T(8,128)S(1)}, f32[64,128]...) custom-call(f32[2560,128]{1,0:T(8,128)S(1)} %get-tuple-element.30.x_, ...), custom_call_target="tpu_custom_call", output_to_operand_aliasing={{0}: (2, {}), {1}: (3, {}), {2}: (4, {}), {3}: (5, {}), {4}... | custom-call | flops 10000000 | bytes 10000000 | tf_op jit(solution)/shard_map/pallas_call | solution.py:391
  13.6 0.0 collective-permute-done.from_west
  13.6 0.0 collective-permute-done.1.from_east
  13.6 0.0 collective-permute-done.2.even_ref
  13.6 0.0 collective-permute-done.3.odd_ref
  13.6 1.8 %shard_map.31 = f32[2560,128]{1,0:T(8,128)} custom-call(f32[2560,128]{1,0:T(8,128)S(1)} %get-tuple-element.30.x_ref, f32[8,128]{1,0:T(8,128)S(1)} %get-tuple-element.31.kmt_ref, f32[64,128]{1,0:T(8,128)S(1)} %get-tuple-element.32.own_ref, f32[2560,128]{1,0:T(8,128)S(1)} %get-tuple-element.44.base_ref, f32[2560,128]{1,0:T(8,128)S(1)} %get-tuple-element.45.cx_ref, ...), custom_call_target="tpu_custom_call" | custom-call | flops 10000000 | bytes 10000000 | tf_op jit(solution)/shard_map/pallas_call | solution.py:391
  (1 shorter events, 0.0 us)
Async XLA Ops:
  1.8 11.8 %collective-permute-start.2 = (f32[328,128]{1,0:T(8,128)S(1)}, f32[328,128]{1,0:T(8,128)S(1)}, u32[]{:S(2)}, u32[]{:S(2)}) collective-permute-start(f32[328,128]{1,0:T(8,128)S(1)} %get-tuple-element.53), channel_id=1, source_target_pairs={{0,1},{1,0},{2,3},{3,2},{4,5},{5,4},{6,7},{7,6},{8,9},{9,8},{10,11... | collective-permute-start | bytes 503816 | tf_op jit(solution)/shard_map/ppermute | solution.py:416
  2.6 11.1 %collective-permute-start.3 = (f32[328,128]{1,0:T(8,128)S(1)}, f32[328,128]{1,0:T(8,128)S(1)}, u32[]{:S(2)}, u32[]{:S(2)}) collective-permute-start(f32[328,128]{1,0:T(8,128)S(1)} %get-tuple-element.54), channel_id=1, source_target_pairs={{1,2},{2,1},{3,31},{5,6},{6,5},{7,27},{9,10},{10,9},{11,23},{13,14... | collective-permute-start | bytes 503816 | tf_op jit(solution)/shard_map/ppermute | solution.py:415
  6.8 6.8 %collective-permute-start = (f32[24,128]{1,0:T(8,128)S(1)}, f32[24,128]{1,0:T(8,128)S(1)}, u32[]{:S(2)}, u32[]{:S(2)}) collective-permute-start(f32[24,128]{1,0:T(8,128)S(1)} %get-tuple-element.51), channel_id=1, source_target_pairs={{0,4},{4,8},{8,12},{12,16},{16,20},{20,24},{24,28},{28,0},{1,5},{5... | collective-permute-start | bytes 36872 | tf_op jit(solution)/shard_map/ppermute | solution.py:412
  7.1 6.5 %collective-permute-start.1 = (f32[24,128]{1,0:T(8,128)S(1)}, f32[24,128]{1,0:T(8,128)S(1)}, u32[]{:S(2)}, u32[]{:S(2)}) collective-permute-start(f32[24,128]{1,0:T(8,128)S(1)} %get-tuple-element.52), channel_id=1, source_target_pairs={{4,0},{8,4},{12,8},{16,12},{20,16},{24,20},{28,24},{0,28},{5,1},{9... | collective-permute-start | bytes 36872 | tf_op jit(solution)/shard_map/ppermute | solution.py:417

commit v4 on v3

v4 whole, which is shorter than its diff:
```python
import functools

import jax
import jax.numpy as jnp
from jax import lax
from jax.experimental import pallas as pl
from jax.experimental.pallas import tpu as pltpu
from jax.sharding import PartitionSpec as P

THERMAL = 0.2
HALINE = 0.8
REDI = 0.1
SKEW = 0.05
SLOPE_MAX = 0.6
SLOPE_WIDTH = 0.2
FACE = 0.25 * (REDI - SKEW)
LEVEL = 0.25 * (REDI + SKEW) / REDI
LOADS = (0.5, 1.0)
STORES = (0.2, 0.4, 0.6, 0.8, 1.0)
UNROLL = 4
EARLY = 5


def taper(slope):
    return slope * 0.5 * (1.0 + jnp.tanh((SLOPE_MAX - jnp.abs(slope)) * (1.0 / SLOPE_WIDTH)))


def lanes_of(shape):
    return lax.broadcasted_iota(jnp.int32, shape, len(shape) - 1)


def rows_of(shape):
    return lax.broadcasted_iota(jnp.int32, shape, len(shape) - 2)


def density_of(heat, salt):
    return HALINE * salt - THERMAL * heat


def as_mask(flag):
    return jnp.where(flag, 1.0, 0.0)


def slope_at(here, there, mask, strat_here, strat_there):
    return taper((here - there) * mask / jnp.maximum(0.5 * (strat_here + strat_there), 1.0))


def level_lists(values, masks):
    diffs = [(values[k + 1] - values[k]) * masks[k] for k in range(len(values) - 1)]
    sums = [diffs[0]] + [a + b for a, b in zip(diffs, diffs[1:])] + [diffs[-1]]
    return diffs, sums


def level_rows(values, mask):
    diffs = (pltpu.roll(values, values.shape[0] - 1, 0) - values) * mask
    return diffs, diffs + pltpu.roll(diffs, 1, 0)


def position():
    lat = lax.axis_index("lat")
    return lax.rem(lat, 2) == 1, lat == 0, lat == lax.axis_size("lat") - 1


def pick(values, index):
    return jnp.take_along_axis(values, index, axis=1, mode="promise_in_bounds")


def pair_of(west, east, cols=128):
    shape = (west.shape[0], cols)
    return jnp.where(lax.rem(lanes_of(shape), 2) == 0, jnp.broadcast_to(west, shape), jnp.broadcast_to(east, shape))


def pack_kernel(dims, x_hbm, kmt_hbm, x_ref, own_ref, east_ref, west_ref, kmt_ref, raw_ref, sems):
    nt, nz, rows, cols, _ = dims
    per = cols // nt
    bounds = chunk_bounds(nt, LOADS)
    kmt_copy = pltpu.make_async_copy(kmt_hbm, raw_ref, sems.at[len(bounds)])
    kmt_copy.start()
    copies = []
    for c, (first, last) in enumerate(bounds):
        part = pl.ds(first * nz * rows, (last - first) * nz * rows)
        copies.append(pltpu.make_async_copy(x_hbm.at[part], x_ref.at[part], sems.at[c]))
        copies[-1].start()
    shape = (rows, cols)
    lane = lanes_of(shape)
    pairs = [jnp.zeros(shape, jnp.float32)] * nz
    for c, (first, last) in enumerate(bounds):
        copies[c].wait()
        for t in range(first, last):
            here = (lane == 2 * t) | (lane == (2 * t - 1) % cols)
            for k in range(nz):
                value = x_ref[pl.ds((t * nz + k) * rows, rows), :]
                pairs[k] = jnp.where(here, pltpu.roll(value, 2 * t, 1) if t else value, pairs[k])
    kmt_copy.wait()
    kmt = raw_ref[...].astype(jnp.float32)
    kmt_ref[...] = kmt
    for k in range(nz):
        own_ref[pl.ds(k * rows, rows), :] = pairs[k]
    for j in range(nz // per + 1):
        east = west = jnp.zeros(shape, jnp.float32)
        for i in range(per):
            k, start = j * per + i, i * nt
            if k > nz:
                break
            index = lax.rem(2 * (lane - start + cols), cols)
            if k == nz:
                side = (jnp.broadcast_to(kmt[:, cols - 1 :], shape), jnp.broadcast_to(kmt[:, :1], shape))
            else:
                side = pick(pairs[k], lax.rem(index + cols - 1, cols)), pick(pairs[k], index)
            east, west = (jnp.where(lane >= start, a, b) for a, b in zip(side, (east, west)))
        east_ref[pl.ds(j * rows, rows), :] = east
        west_ref[pl.ds(j * rows, rows), :] = west


def chunk_bounds(nt, shares):
    ends = [round(nt * share) for share in shares]
    return list(zip([0] + ends, ends))


def pairs_of(west_ref, east_ref, dims, count):
    nt, _, rows, cols, _ = dims
    per = cols // nt
    lane = lanes_of((rows, cols))
    even = lax.rem(lane, 2) == 0
    slot = jnp.where(even, lane // 2, lax.rem(lane + 1, cols) // 2)
    pairs = []
    for k in range(count):
        index = lax.rem(slot + (k % per) * nt, cols)
        part = pl.ds((k // per) * rows, rows)
        pairs.append(jnp.where(even, pick(west_ref[part, :], index), pick(east_ref[part, :], index)))
    return pairs


def early_blocks():
    odd, _, top = position()
    first = lax.axis_index("lon") == 0
    return jnp.where(first & odd & jnp.logical_not(top), EARLY, 0), jnp.where(first & jnp.logical_not(odd), EARLY, 0)


def ends_body(dims, x_ref, kmt_ref, even_ref, odd_ref):
    nt, nz, rows, cols, mirror_color = dims
    odd, _, top = position()

    def put_rows(low, high, start):
        index = lanes_of(low.shape)
        turned = pick(high, jnp.where(top, cols - 1 - index, index))
        for color, ref in ((0, even_ref), (1, odd_ref)):
            up = turned if color == mirror_color else high
            goes_up = odd if color == 1 else jnp.logical_not(odd)
            ref[pl.ds(start, nz), :] = jnp.where(goes_up, up, low)

    kmt = kmt_ref[...]
    put_rows(jnp.broadcast_to(kmt[:1], (nz, cols)), jnp.broadcast_to(kmt[rows - 1 :], (nz, cols)), nt * nz)
    for t in range(nt):
        start = t * nz * rows
        put_rows(x_ref[pl.ds(start, nz, stride=rows), :], x_ref[pl.ds(start + rows - 1, nz, stride=rows), :], t * nz)


def early_kernel(dims, x_ref, kmt_ref, *refs):
    *refs, even_ref, odd_ref = refs
    ends_body(dims, x_ref, kmt_ref, even_ref, odd_ref)
    early, _ = early_blocks()

    @pl.when(early > 0)
    def _():
        coefs_body(dims, x_ref, kmt_ref, *refs[2:])
        inner_body(dims, 0, early, x_ref, kmt_ref, *refs)


def middle_kernel(dims, x_ref, kmt_ref, *refs):
    refs = refs[len(refs) // 2 :]
    _, middle = early_blocks()

    @pl.when(middle > 0)
    def _():
        coefs_body(dims, x_ref, kmt_ref, *refs[2:])
        inner_body(dims, 0, middle, x_ref, kmt_ref, *refs)


def late_kernel(dims, x_ref, kmt_ref, *refs):
    refs = refs[len(refs) // 2 :]
    early, middle = early_blocks()

    @pl.when(early + middle == 0)
    def _():
        coefs_body(dims, x_ref, kmt_ref, *refs[2:])

    inner_body(dims, early + middle, dims[0] // UNROLL, x_ref, kmt_ref, *refs)


def coefs_body(dims, x_ref, kmt_ref, sum_y_ref, inner_ref, dense_ref, cell_w_ref, cell_e_ref, ax_ref, bx_ref, ay_ref, by_ref, p_ref, pw_ref, q_ref, z_ref):
    _, nz, rows, cols, _ = dims
    shape = (rows, cols)
    lane, row = lanes_of(shape), rows_of(shape)
    kmt = kmt_ref[...]
    heat = [x_ref[pl.ds(k * rows, rows), :] for k in range(nz)]
    salt = [x_ref[pl.ds((nz + k) * rows, rows), :] for k in range(nz)]
    density = [density_of(h, s) for h, s in zip(heat, salt)]
    wm = [as_mask(kmt > k + 1) for k in range(nz - 1)]
    kmt_w = pltpu.roll(kmt, 1, 1)
    strat = [0.5 * s for s in level_lists(density, wm)[1]]
    kmt_x = jnp.where(lane == 0, 0.0, jnp.minimum(kmt, kmt_w))
    kmt_y = jnp.where(row == 0, 0.0, jnp.minimum(kmt, pltpu.roll(kmt, 1, 0)))
    sum_x, sum_y = [], []
    for k in range(nz):
        part = pl.ds(k * rows, rows)
        mask = as_mask(kmt_x > k)
        slope = slope_at(density[k], pltpu.roll(density[k], 1, 1), mask, strat[k], pltpu.roll(strat[k], 1, 1))
        ax_ref[part, :] = REDI * mask
        bx_ref[part, :] = FACE * slope
        sum_x.append(slope + pltpu.roll(slope, cols - 1, 1))
        inner_ref[part, :] = pair_of(slope[:, 1:2], slope[:, cols - 1 :])
        mask = as_mask(kmt_y > k)
        slope = slope_at(density[k], pltpu.roll(density[k], 1, 0), mask, strat[k], pltpu.roll(strat[k], 1, 0))
        ay_ref[part, :] = REDI * mask
        by_ref[part, :] = FACE * slope
        sum_y.append(slope + pltpu.roll(slope, rows - 1, 0))
        sum_y_ref[part, :] = sum_y[k]
        dense_ref[part, :] = pair_of(density[k][:, :1], density[k][:, cols - 1 :])
        cell_w_ref[part, :] = jnp.zeros(shape, jnp.float32)
        cell_e_ref[part, :] = jnp.zeros(shape, jnp.float32)
    for k in range(nz - 1):
        part = pl.ds(k * rows, rows)
        level_x, level_y = 0.25 * (sum_x[k] + sum_x[k + 1]), 0.25 * (sum_y[k] + sum_y[k + 1])
        p = LEVEL * level_x * wm[k]
        p_ref[part, :] = p
        pw_ref[part, :] = pltpu.roll(p, 1, 1)
        q_ref[part, :] = LEVEL * level_y * wm[k]
        z_ref[part, :] = REDI * (level_x * level_x + level_y * level_y) * wm[k]


def inner_body(dims, first, last, x_ref, kmt_ref, base_ref, cy_ref, sum_y_ref, inner_ref, dense_ref, cell_w_ref, cell_e_ref,
               ax_ref, bx_ref, ay_ref, by_ref, p_ref, pw_ref, q_ref, z_ref):
    _, nz, rows, cols, _ = dims
    lane = lanes_of((rows, cols))
    kmt = kmt_ref[...]
    kmt_w = pltpu.roll(kmt, 1, 1)
    wm = [as_mask(kmt > k + 1) for k in range(nz - 1)]
    wm_w = [as_mask(kmt_w > k + 1) for k in range(nz - 1)]

    def load(ref, k):
        return ref[pl.ds(k * rows, rows), :]

    def tracer(t):
        base = t * (nz * rows)
        part = lambda k: pl.ds(pl.multiple_of(base + k * rows, rows), rows)
        value = [x_ref[part(k), :] for k in range(nz)]
        beside = [pltpu.roll(v, 1, 1) for v in value]
        diff, total = level_lists(value, wm)
        total_w = level_lists(beside, wm_w)[1]
        at_east, at_west = lane == lax.rem(2 * t + cols - 1, cols), lane == 2 * t + 1
        new, grads, fluxes, cell_y = [], [], [], []
        for k in range(nz):
            grad = load(ax_ref, k) * (value[k] - beside[k])
            grads.append(grad)
            fluxes.append(grad + load(bx_ref, k) * (total[k] + total_w[k]))
            grad = load(ay_ref, k) * (value[k] - pltpu.roll(value[k], 1, 0))
            flux = grad + load(by_ref, k) * (total[k] + pltpu.roll(total[k], 1, 0))
            cell_y.append(grad + pltpu.roll(grad, rows - 1, 0))
            new.append((value[k] - fluxes[k]) + (pltpu.roll(flux, rows - 1, 0) - flux))
        down = down_w = None
        for k in range(nz):
            result, west = new[k], fluxes[k]
            if k > 0:
                result, west = result - down, west - down_w
            if k < nz - 1:
                both_x, both_y = grads[k] + grads[k + 1], cell_y[k] + cell_y[k + 1]
                down = load(p_ref, k) * both_x + load(q_ref, k) * both_y + load(z_ref, k) * diff[k]
                down_w = load(pw_ref, k) * both_x
                result, west = result + down, west + down_w
                cy_ref[part(k), :] = both_y
                moved = pltpu.roll(both_x, lax.rem(2 * t, cols), 1)
                cell_e_ref[pl.ds(k * rows, rows), :] = jnp.where(at_east, moved, load(cell_e_ref, k))
                cell_w_ref[pl.ds(k * rows, rows), :] = jnp.where(at_west, moved, load(cell_w_ref, k))
            else:
                cy_ref[part(k), :] = jnp.zeros((rows, cols), jnp.float32)
            base_ref[part(k), :] = result + pltpu.roll(west, cols - 1, 1)

    def block(i, carry):
        for t in range(UNROLL):
            tracer(i * UNROLL + t)
        return carry

    lax.fori_loop(first, last, block, 0)


def rows_kernel(dims, x_ref, kmt_ref, base_ref, cy_ref, sum_y_ref, even_ref, odd_ref, out_ref):
    nt, nz, rows, cols, _ = dims
    odd, bottom, _ = position()
    kmt = kmt_ref[...]
    flat = (nz, cols)
    level = rows_of(flat).astype(jnp.float32)

    def ends(index):
        a, b = even_ref[pl.ds(index, nz), :], odd_ref[pl.ds(index, nz), :]
        return jnp.where(odd, a, b), jnp.where(odd, b, a)

    def own_rows(ref, t):
        start = t * nz * rows
        return ref[pl.ds(start, nz, stride=rows), :], ref[pl.ds(start + rows - 1, nz, stride=rows), :]

    ghost_kmts = ends(nt * nz)
    ghost_kmts = jnp.where(bottom, 0.0, ghost_kmts[0]), ghost_kmts[1]
    own_kmts = jnp.broadcast_to(kmt[:1], flat), jnp.broadcast_to(kmt[rows - 1 :], flat)
    heats, salts = (own_rows(x_ref, 0), ends(0)), (own_rows(x_ref, 1), ends(nz))
    sums_before = own_rows(sum_y_ref, 0)
    end_coefs = []
    for end, sign in ((0, -1.0), (1, 1.0)):
        kmts = own_kmts[end], ghost_kmts[end]
        wms = [as_mask(k > level + 1.0) for k in kmts]
        mask = as_mask(jnp.minimum(*kmts) > level)
        densities = [density_of(h[end], s[end]) for h, s in zip(heats, salts)]
        strats = [0.5 * level_rows(d, m)[1] for d, m in zip(densities, wms)]
        slope = sign * slope_at(densities[1], densities[0], mask, *strats)
        before = 0.25 * (sums_before[end] + pltpu.roll(sums_before[end], nz - 1, 0))
        change = 0.25 * (slope + pltpu.roll(slope, nz - 1, 0))
        after = before + change
        own_wm = wms[0]
        end_coefs.append((wms, REDI * mask, sign * FACE * slope, sign * LEVEL * after * own_wm, LEVEL * change * own_wm,
                          REDI * change * (before + after) * own_wm))
    for t in range(nt):
        for end in (0, 1):
            wms, a, b, q, q_change, z_change = end_coefs[end]
            here, there = own_rows(x_ref, t)[end], ends(t * nz)[end]
            diff, own_sum = level_rows(here, wms[0])
            grad = a * (there - here)
            gain = grad + b * (own_sum + level_rows(there, wms[1])[1])
            tilt = q * (grad + pltpu.roll(grad, nz - 1, 0)) + q_change * own_rows(cy_ref, t)[end] + z_change * diff
            part = pl.ds(t * nz * rows + (rows - 1 if end else 0), nz, stride=rows)
            out_ref[part, :] = out_ref[part, :] + (gain + (tilt - pltpu.roll(tilt, 1, 0)))


def outer_kernel(dims, kmt_ref, own_ref, base_ref, inner_ref, dense_ref, cell_w_ref, cell_e_ref,
                 from_west, from_east, out_hbm, out_ref, side_ref, sems):
    nt, nz, rows, cols, _ = dims
    shape = (rows, cols)
    lane = lanes_of(shape)
    per = cols // nt
    even = lax.rem(lane, 2) == 0
    kmt = kmt_ref[...]

    def load(ref, k):
        return ref[pl.ds(k * rows, rows), :]

    def spread(k, t):
        start = (k % per) * nt + t
        return pair_of(load(from_west, k // per)[:, start : start + 1], load(from_east, k // per)[:, start : start + 1])

    outward = jnp.where(even, -1.0, 1.0)
    own = [load(own_ref, k) for k in range(nz)]
    ghost = pairs_of(from_west, from_east, dims, nz)
    own_kmt, ghost_kmt = pair_of(kmt[:, :1], kmt[:, cols - 1 :]), spread(nz, 0)
    own_density = [load(dense_ref, k) for k in range(nz)]
    ghost_density = [density_of(spread(k, 0), spread(k, 1)) for k in range(nz)]
    own_wm = [as_mask(own_kmt > k + 1) for k in range(nz - 1)]
    ghost_wm = [as_mask(ghost_kmt > k + 1) for k in range(nz - 1)]
    side_mask = [as_mask(jnp.minimum(own_kmt, ghost_kmt) > k) for k in range(nz)]
    own_strat = level_lists(own_density, own_wm)[1]
    ghost_strat = level_lists(ghost_density, ghost_wm)[1]
    side_slope = [
        outward * slope_at(ghost_density[k], own_density[k], side_mask[k], 0.5 * own_strat[k], 0.5 * ghost_strat[k])
        for k in range(nz)
    ]
    own_diff, own_sum = level_lists(own, own_wm)
    ghost_sum = level_lists(ghost, ghost_wm)[1]
    grad = [REDI * side_mask[k] * (ghost[k] - own[k]) for k in range(nz)]
    flux = [grad[k] + outward * FACE * side_slope[k] * (own_sum[k] + ghost_sum[k]) for k in range(nz)]
    tilt = []
    for k in range(nz - 1):
        before = 0.25 * (load(inner_ref, k) + load(inner_ref, k + 1))
        change = 0.25 * (side_slope[k] + side_slope[k + 1])
        after = before + change
        inner = jnp.where(even, pltpu.roll(load(cell_w_ref, k), cols - 1, 1), load(cell_e_ref, k))
        across = after * outward * (grad[k] + grad[k + 1]) + change * inner
        along = change * (before + after) * own_diff[k]
        tilt.append(own_wm[k] * (LEVEL * across + REDI * along))
    for k in range(nz):
        added = flux[k]
        if k < nz - 1:
            added = added + tilt[k]
        if k > 0:
            added = added - tilt[k - 1]
        side_ref[pl.ds(k * rows, rows), :] = added
    outer = (lane == 0) | (lane == cols - 1)
    copies = []
    for c, (first, last) in enumerate(chunk_bounds(nt, STORES)):
        for t in range(first, last):
            for k in range(nz):
                part = pl.ds((t * nz + k) * rows, rows)
                side = load(side_ref, k)
                side = pltpu.roll(side, cols - 2 * t, 1) if t else side
                out_ref[part, :] = base_ref[part, :] + jnp.where(outer, side, 0.0)
        part = pl.ds(first * nz * rows, (last - first) * nz * rows)
        copies.append(pltpu.make_async_copy(out_ref.at[part], out_hbm.at[part], sems.at[c]))
        copies[-1].start()
    for copy in copies:
        copy.wait()


def row_pairs(color, lons, lats):
    pairs = []
    for lon in range(lons):
        for lat in range(lats - 1):
            if lat % 2 == color:
                pairs += [(lon * lats + lat, lon * lats + lat + 1), (lon * lats + lat + 1, lon * lats + lat)]
        if (lats - 1) % 2 == color:
            pairs.append((lon * lats + lats - 1, (lons - 1 - lon) * lats + lats - 1))
    free_in = sorted(set(range(lons * lats)) - {b for _, b in pairs})
    free_out = set(range(lons * lats)) - {a for a, _ in pairs}
    for target in free_in:
        lon, lat = divmod(target, lats)
        source = (lon ^ 1 if lons % 2 == 0 else (lon + 1) % lons) * lats + lat
        assert source in free_out
        pairs.append((source, target))
    return pairs


def local(tracers, kmt):
    nt, nz, rows, cols = tracers.shape
    lons, lats = lax.axis_size("lon"), lax.axis_size("lat")
    dims = (nt, nz, rows, cols, (lats - 1) % 2)
    packed = ((nz // (cols // nt) + 1) * rows, cols)
    edge = (nt * nz + nz, cols)
    level, block = (nz * rows, cols), (nt * nz * rows, cols)
    vmem, anywhere = pl.BlockSpec(memory_space=pltpu.VMEM), pl.BlockSpec(memory_space=pl.ANY)

    def call(kernel, inputs, out_shape, scratch, flops, specs=None, aliases={}):
        out = [pltpu.VMEM(s, jnp.float32) for s in out_shape] if specs is None else out_shape
        if specs is None:
            specs = [vmem] * len(out_shape)
        near = [pltpu.with_memory_space_constraint(a, pltpu.HBM if a is x or a is kmt else pltpu.VMEM) for a in inputs]
        return pl.pallas_call(
            functools.partial(kernel, dims),
            out_shape=out,
            in_specs=[anywhere if a is x or a is kmt else vmem for a in inputs],
            out_specs=specs,
            scratch_shapes=scratch,
            input_output_aliases=aliases,
            cost_estimate=pl.CostEstimate(flops=flops, bytes_accessed=flops, transcendentals=0),
            compiler_params=pltpu.CompilerParams(vmem_limit_bytes=16 * 2**20),
        )(*near)

    x = tracers.reshape(block)
    near, own, east, west, near_kmt = call(
        pack_kernel,
        (x, kmt),
        (block, level, packed, packed, (rows, cols)),
        [pltpu.VMEM((rows, cols), jnp.int32), pltpu.SemaphoreType.DMA((len(LOADS) + 1,))],
        1000000,
    )
    ring = [(i, (i + 1) % lons) for i in range(lons)]
    from_west = lax.ppermute(east, "lon", ring)
    shapes = (block,) * 2 + (level,) * 13
    *inner, even, odd = call(early_kernel, (near, near_kmt), (*shapes, edge, edge), [], 10000000)
    from_odd = lax.ppermute(odd, ("lon", "lat"), row_pairs(1, lons, lats))
    aliases = {2 + i: i for i in range(len(shapes))}
    inner = call(middle_kernel, (near, near_kmt, *inner), shapes, [], 10000000, aliases=aliases)
    from_even = lax.ppermute(even, ("lon", "lat"), row_pairs(0, lons, lats))
    from_east = lax.ppermute(west, "lon", [(b, a) for a, b in ring])
    inner = call(late_kernel, (near, near_kmt, *inner), shapes, [], 10000000, aliases=aliases)
    base, cy, sum_y, inner_slope, dense, cell_w, cell_e = inner[:7]
    ends = (near, near_kmt, base, cy, sum_y, from_even, from_odd)
    (base,) = call(rows_kernel, ends, (block,), [], 1000000, aliases={2: 0})
    out = call(
        outer_kernel,
        (near_kmt, own, base, inner_slope, dense, cell_w, cell_e, from_west, from_east),
        jax.ShapeDtypeStruct(block, jnp.float32),
        [pltpu.VMEM(block, jnp.float32), pltpu.VMEM(level, jnp.float32), pltpu.SemaphoreType.DMA((len(STORES),))],
        10000000,
        anywhere,
    )
    return out.reshape(tracers.shape)


def solution(mesh):
    return jax.shard_map(
        local,
        mesh=mesh,
        in_specs=(P(None, None, "lat", "lon"), P("lat", "lon")),
        out_specs=P(None, None, "lat", "lon"),
        check_vma=False,
    )
```

time: 15.6 us -> 15.8 us (1.013)
    pallas_call x4 -> x6, Pallas kernels: 6.26 us -> 6.41 us  [call(): pl.pallas_call(functools.partial(kernel, dims), out_shape=out, in_specs=[...]
  transfers between devices with their start and end apart: 4 -> 4, of which waited for: 0 -> 0; matrix products, arithmetic and copies ran while one was open for 0% -> 0% of each run, Pallas kernels for 17% -> 20%
where the time goes in v4:
time: 15.8 us; the launch traced here: 15.6 us
  starting transfers between devices  9.15 us (58%)
  Pallas kernels  6.41 us (41%)
    pallas_call x6, Pallas kernels, call(): pl.pallas_call(functools.partial(kernel, dims), out_shape=out, in_specs=[...  6.41 us
    ppermute x1, starting transfers between devices, local(): from_odd = lax.ppermute(odd, ('lon', 'lat'), row_pairs(1, lons, lats))  4.25 us
    ppermute x1, starting transfers between devices, local(): from_east = lax.ppermute(west, 'lon', [(b, a) for a, b in ring])  3.91 us
    ppermute x1, starting transfers between devices, local(): from_even = lax.ppermute(even, ('lon', 'lat'), row_pairs(0, lons, lats))  0.74 us
  transfers between devices with their start and end apart: 4, of which 0 were waited for; matrix products, arithmetic and copies ran while one was open for 0% of the time, Pallas kernels for 20%

profile of v4, /device:TPU:5, one launch (start us, length us, event | category | flops | bytes accessed | tf_op | source)
XLA Modules:
  0.0 15.6 jit_solution(9566539842846025022)
XLA Ops:
  0.0 1.7 %shard_map.28 = (f32[2560,128]{1,0:T(8,128)S(1)}, f32[64,128]{1,0:T(8,128)S(1)}, f32[24,128]{1,0:T(8,128)S(1)}, f32[24,128]{1,0:T(8,128)S(1)}, f32[8,128]{1,0:T(8,128)S(1)}) custom-call(f32[2560,128]{1,0:T(8,128)} %bitcast.2, s32[8,128]{1,0:T(8,128)} %kmt_hbm.1), custom_call_target="tpu_custom_call" | custom-call | flops 1000000 | bytes 1000000 | tf_op jit(solution)/shard_map/pallas_call | solution.py:432
  1.7 0.1 shard_map.29
  1.9 0.7 %collective-permute-start = (f32[328,128]{1,0:T(8,128)S(1)}, f32[328,128]{1,0:T(8,128)S(1)}, u32[]{:S(2)}, u32[]{:S(2)}) collective-permute-start(f32[328,128]{1,0:T(8,128)S(1)} %get-tuple-element.85), channel_id=1, source_target_pairs={{0,1},{1,0},{2,3},{3,2},{4,5},{5,4},{6,7},{7,6},{8,9},{9,8},{10,11... | collective-permute-start | bytes 503816 | tf_op jit(solution)/shard_map/ppermute | solution.py:458
  2.6 4.2 %collective-permute-start.1 = (f32[328,128]{1,0:T(8,128)S(1)}, f32[328,128]{1,0:T(8,128)S(1)}, u32[]{:S(2)}, u32[]{:S(2)}) collective-permute-start(f32[328,128]{1,0:T(8,128)S(1)} %get-tuple-element.86), channel_id=1, source_target_pairs={{1,2},{2,1},{3,31},{5,6},{6,5},{7,27},{9,10},{10,9},{11,23},{13,14... | collective-permute-start | bytes 503816 | tf_op jit(solution)/shard_map/ppermute | solution.py:455
  6.8 0.3 %collective-permute-start.2 = (f32[24,128]{1,0:T(8,128)S(1)}, f32[24,128]{1,0:T(8,128)S(1)}, u32[]{:S(2)}, u32[]{:S(2)}) collective-permute-start(f32[24,128]{1,0:T(8,128)S(1)} %get-tuple-element.91), channel_id=1, source_target_pairs={{0,4},{4,8},{8,12},{12,16},{16,20},{20,24},{24,28},{28,0},{1,5},{5... | collective-permute-start | bytes 36872 | tf_op jit(solution)/shard_map/ppermute | solution.py:452
  7.1 3.9 %collective-permute-start.3 = (f32[24,128]{1,0:T(8,128)S(1)}, f32[24,128]{1,0:T(8,128)S(1)}, u32[]{:S(2)}, u32[]{:S(2)}) collective-permute-start(f32[24,128]{1,0:T(8,128)S(1)} %get-tuple-element.92), channel_id=1, source_target_pairs={{4,0},{8,4},{12,8},{16,12},{20,16},{24,20},{28,24},{0,28},{5,1},{9... | collective-permute-start | bytes 36872 | tf_op jit(solution)/shard_map/ppermute | solution.py:459
  11.0 2.8 %shard_map.31 = (f32[2560,128]{1,0:T(8,128)S(1)}, f32[2560,128]{1,0:T(8,128)S(1)}, f32[64,128]{1,0:T(8,128)S(1)}, f32[64,128]{1,0:T(8,128)S(1)}, f32[64,128]{1,0...) custom-call(f32[2560,128]{1,0:T(8,128)S(1)} %get-tuple-element.51.x_, ...), custom_call_target="tpu_custom_call", output_to_operand_aliasing={{0}: (2, {}), {1}: (3, {}), {2}: (4, {}), {3}: (5, {}), {4}... | custom-call | flops 10000000 | bytes 10000000 | tf_op jit(solution)/shard_map/pallas_call | solution.py:432
  13.8 0.0 collective-permute-done.even_ref
  13.8 0.0 collective-permute-done.1.odd_ref
  13.8 0.4 %shard_map.32.base_ref = f32[2560,128]{1,0:T(8,128)S(1)} custom-call(f32[2560,128]{1,0:T(8,128)S(1)} %get-tuple-element.51.x_ref, f32[8,128]{1,0:T(8,128)S(1)} %get-tuple-element.49.kmt_ref, f32[2560,128]{1,0:T(8,128)S(1)} %get-tuple-element.82.base_ref, f32[2560,128]{1,0:T(8,128)S(1)} %get-tuple-element.83.cy_ref, ...), custom_call_target="tpu_custom_call", output_to_operand_aliasing={{}: (2, {})} | custom-call | flops 1000000 | bytes 1000000 | tf_op jit(solution)/shard_map/pallas_call | solution.py:432
  14.2 0.0 collective-permute-done.2.from_west
  14.2 0.0 collective-permute-done.3.from_east
  14.2 1.4 %shard_map.33 = f32[2560,128]{1,0:T(8,128)} custom-call(f32[8,128]{1,0:T(8,128)S(1)} %get-tuple-element.49.kmt_ref, f32[64,128]{1,0:T(8,128)S(1)} %get-tuple-element.50.own_ref, f32[2560,128]{1,0:T(8,128)S(1)} %shard_map.32.base_ref, f32[64,128]{1,0:T(8,128)S(1)} %get-tuple-element.87.inner_ref, f32[64,128]{1,0:T(8,128)S(1)} %get-tuple-element.88.dense_ref, ...), custom_call_target="tpu_custom_call" | custom-call | flops 10000000 | bytes 10000000 | tf_op jit(solution)/shard_map/pallas_call | solution.py:432
  (1 shorter events, 0.0 us)
Async XLA Ops:
  1.9 11.9 %collective-permute-start = (f32[328,128]{1,0:T(8,128)S(1)}, f32[328,128]{1,0:T(8,128)S(1)}, u32[]{:S(2)}, u32[]{:S(2)}) collective-permute-start(f32[328,128]{1,0:T(8,128)S(1)} %get-tuple-element.85), channel_id=1, source_target_pairs={{0,1},{1,0},{2,3},{3,2},{4,5},{5,4},{6,7},{7,6},{8,9},{9,8},{10,11... | collective-permute-start | bytes 503816 | tf_op jit(solution)/shard_map/ppermute | solution.py:458
  2.6 11.2 %collective-permute-start.1 = (f32[328,128]{1,0:T(8,128)S(1)}, f32[328,128]{1,0:T(8,128)S(1)}, u32[]{:S(2)}, u32[]{:S(2)}) collective-permute-start(f32[328,128]{1,0:T(8,128)S(1)} %get-tuple-element.86), channel_id=1, source_target_pairs={{1,2},{2,1},{3,31},{5,6},{6,5},{7,27},{9,10},{10,9},{11,23},{13,14... | collective-permute-start | bytes 503816 | tf_op jit(solution)/shard_map/ppermute | solution.py:455
  6.8 7.3 %collective-permute-start.2 = (f32[24,128]{1,0:T(8,128)S(1)}, f32[24,128]{1,0:T(8,128)S(1)}, u32[]{:S(2)}, u32[]{:S(2)}) collective-permute-start(f32[24,128]{1,0:T(8,128)S(1)} %get-tuple-element.91), channel_id=1, source_target_pairs={{0,4},{4,8},{8,12},{12,16},{16,20},{20,24},{24,28},{28,0},{1,5},{5... | collective-permute-start | bytes 36872 | tf_op jit(solution)/shard_map/ppermute | solution.py:452
  7.1 7.1 %collective-permute-start.3 = (f32[24,128]{1,0:T(8,128)S(1)}, f32[24,128]{1,0:T(8,128)S(1)}, u32[]{:S(2)}, u32[]{:S(2)}) collective-permute-start(f32[24,128]{1,0:T(8,128)S(1)} %get-tuple-element.92), channel_id=1, source_target_pairs={{4,0},{8,4},{12,8},{16,12},{20,16},{24,20},{28,24},{0,28},{5,1},{9... | collective-permute-start | bytes 36872 | tf_op jit(solution)/shard_map/ppermute | solution.py:459

commit v5 on v4

--- a/solution.py
+++ b/solution.py
@@ -18,7 +18,8 @@
 LOADS = (0.5, 1.0)
 STORES = (0.2, 0.4, 0.6, 0.8, 1.0)
 UNROLL = 4
-EARLY = 5
+EVEN = (2, 6)
+ODD = (5, 5)
 
 
 def taper(slope):
@@ -70,8 +71,8 @@
     return jnp.where(lax.rem(lanes_of(shape), 2) == 0, jnp.broadcast_to(west, shape), jnp.broadcast_to(east, shape))
 
 
-def pack_kernel(dims, x_hbm, kmt_hbm, x_ref, own_ref, east_ref, west_ref, kmt_ref, raw_ref, sems):
-    nt, nz, rows, cols, _ = dims
+def pack_kernel(dims, x_hbm, kmt_hbm, x_ref, own_ref, east_ref, west_ref, kmt_ref, even_ref, odd_ref, raw_ref, sems):
+    nt, nz, rows, cols, mirror_color = dims
     per = cols // nt
     bounds = chunk_bounds(nt, LOADS)
     kmt_copy = pltpu.make_async_copy(kmt_hbm, raw_ref, sems.at[len(bounds)])
@@ -83,6 +84,16 @@
         copies[-1].start()
     shape = (rows, cols)
     lane = lanes_of(shape)
+    odd, _, top = position()
+
+    def put_rows(low, high, start):
+        index = lanes_of(low.shape)
+        turned = pick(high, jnp.where(top, cols - 1 - index, index))
+        for color, ref in ((0, even_ref), (1, odd_ref)):
+            up = turned if color == mirror_color else high
+            goes_up = odd if color == 1 else jnp.logical_not(odd)
+            ref[pl.ds(start, nz), :] = jnp.where(goes_up, up, low)
+
     pairs = [jnp.zeros(shape, jnp.float32)] * nz
     for c, (first, last) in enumerate(bounds):
         copies[c].wait()
@@ -91,9 +102,13 @@
             for k in range(nz):
                 value = x_ref[pl.ds((t * nz + k) * rows, rows), :]
                 pairs[k] = jnp.where(here, pltpu.roll(value, 2 * t, 1) if t else value, pairs[k])
+        for t in range(first, last):
+            start = t * nz * rows
+            put_rows(x_ref[pl.ds(start, nz, stride=rows), :], x_ref[pl.ds(start + rows - 1, nz, stride=rows), :], t * nz)
     kmt_copy.wait()
     kmt = raw_ref[...].astype(jnp.float32)
     kmt_ref[...] = kmt
+    put_rows(jnp.broadcast_to(kmt[:1], (nz, cols)), jnp.broadcast_to(kmt[rows - 1 :], (nz, cols)), nt * nz)
     for k in range(nz):
         own_ref[pl.ds(k * rows, rows), :] = pairs[k]
     for j in range(nz // per + 1):
@@ -133,59 +148,36 @@
 
 def early_blocks():
     odd, _, top = position()
-    first = lax.axis_index("lon") == 0
-    return jnp.where(first & odd & jnp.logical_not(top), EARLY, 0), jnp.where(first & jnp.logical_not(odd), EARLY, 0)
-
-
-def ends_body(dims, x_ref, kmt_ref, even_ref, odd_ref):
-    nt, nz, rows, cols, mirror_color = dims
-    odd, _, top = position()
-
-    def put_rows(low, high, start):
-        index = lanes_of(low.shape)
-        turned = pick(high, jnp.where(top, cols - 1 - index, index))
-        for color, ref in ((0, even_ref), (1, odd_ref)):
-            up = turned if color == mirror_color else high
-            goes_up = odd if color == 1 else jnp.logical_not(odd)
-            ref[pl.ds(start, nz), :] = jnp.where(goes_up, up, low)
-
-    kmt = kmt_ref[...]
-    put_rows(jnp.broadcast_to(kmt[:1], (nz, cols)), jnp.broadcast_to(kmt[rows - 1 :], (nz, cols)), nt * nz)
-    for t in range(nt):
-        start = t * nz * rows
-        put_rows(x_ref[pl.ds(start, nz, stride=rows), :], x_ref[pl.ds(start + rows - 1, nz, stride=rows), :], t * nz)
+    first = (lax.axis_index("lon") == 0) & jnp.logical_not(top)
+    return tuple(jnp.where(first, jnp.where(odd, b, a), 0) for a, b in zip(EVEN, ODD))
 
 
 def early_kernel(dims, x_ref, kmt_ref, *refs):
-    *refs, even_ref, odd_ref = refs
-    ends_body(dims, x_ref, kmt_ref, even_ref, odd_ref)
+    *refs, turned_ref = refs
     early, _ = early_blocks()
 
     @pl.when(early > 0)
     def _():
         coefs_body(dims, x_ref, kmt_ref, *refs[2:])
-        inner_body(dims, 0, early, x_ref, kmt_ref, *refs)
+        inner_body(dims, 0, early, turned_ref, x_ref, kmt_ref, *refs)
 
 
 def middle_kernel(dims, x_ref, kmt_ref, *refs):
+    *refs, turned_ref = refs
     refs = refs[len(refs) // 2 :]
-    _, middle = early_blocks()
-
-    @pl.when(middle > 0)
+    inner_body(dims, *early_blocks(), turned_ref, x_ref, kmt_ref, *refs)
+
+
+def late_kernel(dims, x_ref, kmt_ref, *refs):
+    *refs, turned_ref = refs
+    refs = refs[len(refs) // 2 :]
+    _, done = early_blocks()
+
+    @pl.when(done == 0)
     def _():
         coefs_body(dims, x_ref, kmt_ref, *refs[2:])
-        inner_body(dims, 0, middle, x_ref, kmt_ref, *refs)
-
-
-def late_kernel(dims, x_ref, kmt_ref, *refs):
-    refs = refs[len(refs) // 2 :]
-    early, middle = early_blocks()
-
-    @pl.when(early + middle == 0)
-    def _():
-        coefs_body(dims, x_ref, kmt_ref, *refs[2:])
-
-    inner_body(dims, early + middle, dims[0] // UNROLL, x_ref, kmt_ref, *refs)
+
+    inner_body(dims, done, dims[0] // UNROLL, turned_ref, x_ref, kmt_ref, *refs)
 
 
 def coefs_body(dims, x_ref, kmt_ref, sum_y_ref, inner_ref, dense_ref, cell_w_ref, cell_e_ref, ax_ref, bx_ref, ay_ref, by_ref, p_ref, pw_ref, q_ref, z_ref):
@@ -229,23 +221,25 @@
         z_ref[part, :] = REDI * (level_x * level_x + level_y * level_y) * wm[k]
 
 
-def inner_body(dims, first, last, x_ref, kmt_ref, base_ref, cy_ref, sum_y_ref, inner_ref, dense_ref, cell_w_ref, cell_e_ref,
+def inner_body(dims, first, last, turned_ref, x_ref, kmt_ref, base_ref, cy_ref, sum_y_ref, inner_ref, dense_ref, cell_w_ref, cell_e_ref,
                ax_ref, bx_ref, ay_ref, by_ref, p_ref, pw_ref, q_ref, z_ref):
-    _, nz, rows, cols, _ = dims
+    nt, nz, rows, cols, _ = dims
     lane = lanes_of((rows, cols))
-    kmt = kmt_ref[...]
-    kmt_w = pltpu.roll(kmt, 1, 1)
-    wm = [as_mask(kmt > k + 1) for k in range(nz - 1)]
-    wm_w = [as_mask(kmt_w > k + 1) for k in range(nz - 1)]
 
     def load(ref, k):
         return ref[pl.ds(k * rows, rows), :]
 
-    def tracer(t):
+    def turn(i):
+        for j in range(UNROLL * nz):
+            part = pl.ds(pl.multiple_of((i * UNROLL * nz + j) * rows, rows), rows)
+            turned_ref[lax.rem(i, 2), pl.ds(j * rows, rows), :] = pltpu.roll(x_ref[part, :], 1, 1)
+
+    def tracer(i, j, wm, wm_w):
+        t = i * UNROLL + j
         base = t * (nz * rows)
         part = lambda k: pl.ds(pl.multiple_of(base + k * rows, rows), rows)
         value = [x_ref[part(k), :] for k in range(nz)]
-        beside = [pltpu.roll(v, 1, 1) for v in value]
+        beside = [turned_ref[lax.rem(i, 2), pl.ds((j * nz + k) * rows, rows), :] for k in range(nz)]
         diff, total = level_lists(value, wm)
         total_w = level_lists(beside, wm_w)[1]
         at_east, at_west = lane == lax.rem(2 * t + cols - 1, cols), lane == 2 * t + 1
@@ -276,12 +270,21 @@
                 cy_ref[part(k), :] = jnp.zeros((rows, cols), jnp.float32)
             base_ref[part(k), :] = result + pltpu.roll(west, cols - 1, 1)
 
-    def block(i, carry):
-        for t in range(UNROLL):
-            tracer(i * UNROLL + t)
-        return carry
-
-    lax.fori_loop(first, last, block, 0)
+    @pl.when(first < last)
+    def _():
+        kmt = kmt_ref[...]
+        kmt_w = pltpu.roll(kmt, 1, 1)
+        wm = [as_mask(kmt > k + 1) for k in range(nz - 1)]
+        wm_w = [as_mask(kmt_w > k + 1) for k in range(nz - 1)]
+        turn(first)
+
+        def step(i, carry):
+            for j in range(UNROLL):
+                tracer(i, j, wm, wm_w)
+            turn(jnp.minimum(i + 1, nt // UNROLL - 1))
+            return carry
+
+        lax.fori_loop(first, last, step, 0)
 
 
 def rows_kernel(dims, x_ref, kmt_ref, base_ref, cy_ref, sum_y_ref, even_ref, odd_ref, out_ref):
@@ -441,23 +444,24 @@
         )(*near)
 
     x = tracers.reshape(block)
-    near, own, east, west, near_kmt = call(
+    near, own, east, west, near_kmt, even, odd = call(
         pack_kernel,
         (x, kmt),
-        (block, level, packed, packed, (rows, cols)),
+        (block, level, packed, packed, (rows, cols), edge, edge),
         [pltpu.VMEM((rows, cols), jnp.int32), pltpu.SemaphoreType.DMA((len(LOADS) + 1,))],
         1000000,
     )
     ring = [(i, (i + 1) % lons) for i in range(lons)]
     from_west = lax.ppermute(east, "lon", ring)
     shapes = (block,) * 2 + (level,) * 13
-    *inner, even, odd = call(early_kernel, (near, near_kmt), (*shapes, edge, edge), [], 10000000)
+    turned = [pltpu.VMEM((2, UNROLL * nz * rows, cols), jnp.float32)]
+    inner = call(early_kernel, (near, near_kmt), shapes, turned, 10000000)
     from_odd = lax.ppermute(odd, ("lon", "lat"), row_pairs(1, lons, lats))
     aliases = {2 + i: i for i in range(len(shapes))}
-    inner = call(middle_kernel, (near, near_kmt, *inner), shapes, [], 10000000, aliases=aliases)
+    inner = call(middle_kernel, (near, near_kmt, *inner), shapes, turned, 10000000, aliases=aliases)
     from_even = lax.ppermute(even, ("lon", "lat"), row_pairs(0, lons, lats))
     from_east = lax.ppermute(west, "lon", [(b, a) for a, b in ring])
-    inner = call(late_kernel, (near, near_kmt, *inner), shapes, [], 10000000, aliases=aliases)
+    inner = call(late_kernel, (near, near_kmt, *inner), shapes, turned, 10000000, aliases=aliases)
     base, cy, sum_y, inner_slope, dense, cell_w, cell_e = inner[:7]
     ends = (near, near_kmt, base, cy, sum_y, from_even, from_odd)
     (base,) = call(rows_kernel, ends, (block,), [], 1000000, aliases={2: 0})

time: 15.8 us -> 15.3 us (0.968)
  Pallas kernels: 6.41 us -> 5.93 us
    pallas_call x6, Pallas kernels: 6.41 us -> 5.93 us  [call(): pl.pallas_call(functools.partial(kernel, dims), out_shape=out, in_specs=[...]
  transfers between devices with their start and end apart: 4 -> 4, of which waited for: 0 -> 0; matrix products, arithmetic and copies ran while one was open for 0% -> 0% of each run, Pallas kernels for 20% -> 18%
where the time goes in v5:
time: 15.3 us; the launch traced here: 15.2 us
  starting transfers between devices  9.15 us (60%)
  Pallas kernels  5.93 us (39%)
    pallas_call x6, Pallas kernels, call(): pl.pallas_call(functools.partial(kernel, dims), out_shape=out, in_specs=[...  5.93 us
    ppermute x1, starting transfers between devices, local(): from_odd = lax.ppermute(odd, ('lon', 'lat'), row_pairs(1, lons, lats))  4.25 us
    ppermute x1, starting transfers between devices, local(): from_east = lax.ppermute(west, 'lon', [(b, a) for a, b in ring])  3.91 us
    ppermute x1, starting transfers between devices, local(): from_even = lax.ppermute(even, ('lon', 'lat'), row_pairs(0, lons, lats))  0.74 us
  transfers between devices with their start and end apart: 4, of which 0 were waited for; matrix products, arithmetic and copies ran while one was open for 0% of the time, Pallas kernels for 18%

profile of v5, /device:TPU:5, one launch (start us, length us, event | category | flops | bytes accessed | tf_op | source)
XLA Modules:
  0.0 15.2 jit_solution(3505451425887647821)
XLA Ops:
  0.0 1.8 %shard_map.28 = (f32[2560,128]{1,0:T(8,128)S(1)}, f32[64,128]{1,0:T(8,128)S(1)}, f32[24,128]{1,0:T(8,128)S(1)}, f32[24,128]{1,0:T(8,128)S(1)}, f32[8,128]{1,0:T(...) custom-call(f32[2560,128]{1,0:T(8,128)} %bitcast.2, s32[8,128]{1,0:T(8,128)} %kmt_hbm.1), custom_call_target="tpu_custom_call" | custom-call | flops 1000000 | bytes 1000000 | tf_op jit(solution)/shard_map/pallas_call | solution.py:435
  1.8 0.7 %collective-permute-start = (f32[328,128]{1,0:T(8,128)S(1)}, f32[328,128]{1,0:T(8,128)S(1)}, u32[]{:S(2)}, u32[]{:S(2)}) collective-permute-start(f32[328,128]{1,0:T(8,128)S(1)} %get-tuple-element.85), channel_id=1, source_target_pairs={{0,1},{1,0},{2,3},{3,2},{4,5},{5,4},{6,7},{7,6},{8,9},{9,8},{10,11... | collective-permute-start | bytes 503816 | tf_op jit(solution)/shard_map/ppermute | solution.py:462
  2.5 4.2 %collective-permute-start.1 = (f32[328,128]{1,0:T(8,128)S(1)}, f32[328,128]{1,0:T(8,128)S(1)}, u32[]{:S(2)}, u32[]{:S(2)}) collective-permute-start(f32[328,128]{1,0:T(8,128)S(1)} %get-tuple-element.86), channel_id=1, source_target_pairs={{1,2},{2,1},{3,31},{5,6},{6,5},{7,27},{9,10},{10,9},{11,23},{13,14... | collective-permute-start | bytes 503816 | tf_op jit(solution)/shard_map/ppermute | solution.py:459
  6.8 0.3 %collective-permute-start.2 = (f32[24,128]{1,0:T(8,128)S(1)}, f32[24,128]{1,0:T(8,128)S(1)}, u32[]{:S(2)}, u32[]{:S(2)}) collective-permute-start(f32[24,128]{1,0:T(8,128)S(1)} %get-tuple-element.91), channel_id=1, source_target_pairs={{0,4},{4,8},{8,12},{12,16},{16,20},{20,24},{24,28},{28,0},{1,5},{5... | collective-permute-start | bytes 36872 | tf_op jit(solution)/shard_map/ppermute | solution.py:455
  7.0 3.9 %collective-permute-start.3 = (f32[24,128]{1,0:T(8,128)S(1)}, f32[24,128]{1,0:T(8,128)S(1)}, u32[]{:S(2)}, u32[]{:S(2)}) collective-permute-start(f32[24,128]{1,0:T(8,128)S(1)} %get-tuple-element.92), channel_id=1, source_target_pairs={{4,0},{8,4},{12,8},{16,12},{20,16},{24,20},{28,24},{0,28},{5,1},{9... | collective-permute-start | bytes 36872 | tf_op jit(solution)/shard_map/ppermute | solution.py:463
  10.9 2.4 %shard_map.31 = (f32[2560,128]{1,0:T(8,128)S(1)}, f32[2560,128]{1,0:T(8,128)S(1)}, f32[64,128]{1,0:T(8,128)S(1)}, f32[64,128]{1,0:T(8,128)S(1)}, f32[64,128]{1,0...) custom-call(f32[2560,128]{1,0:T(8,128)S(1)} %get-tuple-element.51.x_, ...), custom_call_target="tpu_custom_call", output_to_operand_aliasing={{0}: (2, {}), {1}: (3, {}), {2}: (4, {}), {3}: (5, {}), {4}... | custom-call | flops 10000000 | bytes 10000000 | tf_op jit(solution)/shard_map/pallas_call | solution.py:435
  13.3 0.0 collective-permute-done.even_ref
  13.3 0.0 collective-permute-done.1.odd_ref
  13.3 0.4 %shard_map.32.base_ref = f32[2560,128]{1,0:T(8,128)S(1)} custom-call(f32[2560,128]{1,0:T(8,128)S(1)} %get-tuple-element.51.x_ref, f32[8,128]{1,0:T(8,128)S(1)} %get-tuple-element.49.kmt_ref, f32[2560,128]{1,0:T(8,128)S(1)} %get-tuple-element.82.base_ref, f32[2560,128]{1,0:T(8,128)S(1)} %get-tuple-element.83.cy_ref, ...), custom_call_target="tpu_custom_call", output_to_operand_aliasing={{}: (2, {})} | custom-call | flops 1000000 | bytes 1000000 | tf_op jit(solution)/shard_map/pallas_call | solution.py:435
  13.7 0.0 collective-permute-done.2.from_west
  13.7 0.0 collective-permute-done.3.from_east
  13.7 1.4 %shard_map.33 = f32[2560,128]{1,0:T(8,128)} custom-call(f32[8,128]{1,0:T(8,128)S(1)} %get-tuple-element.49.kmt_ref, f32[64,128]{1,0:T(8,128)S(1)} %get-tuple-element.50.own_ref, f32[2560,128]{1,0:T(8,128)S(1)} %shard_map.32.base_ref, f32[64,128]{1,0:T(8,128)S(1)} %get-tuple-element.87.inner_ref, f32[64,128]{1,0:T(8,128)S(1)} %get-tuple-element.88.dense_ref, ...), custom_call_target="tpu_custom_call" | custom-call | flops 10000000 | bytes 10000000 | tf_op jit(solution)/shard_map/pallas_call | solution.py:435
  (2 shorter events, 0.0 us)
Async XLA Ops:
  1.8 11.5 %collective-permute-start = (f32[328,128]{1,0:T(8,128)S(1)}, f32[328,128]{1,0:T(8,128)S(1)}, u32[]{:S(2)}, u32[]{:S(2)}) collective-permute-start(f32[328,128]{1,0:T(8,128)S(1)} %get-tuple-element.85), channel_id=1, source_target_pairs={{0,1},{1,0},{2,3},{3,2},{4,5},{5,4},{6,7},{7,6},{8,9},{9,8},{10,11... | collective-permute-start | bytes 503816 | tf_op jit(solution)/shard_map/ppermute | solution.py:462
  2.5 10.8 %collective-permute-start.1 = (f32[328,128]{1,0:T(8,128)S(1)}, f32[328,128]{1,0:T(8,128)S(1)}, u32[]{:S(2)}, u32[]{:S(2)}) collective-permute-start(f32[328,128]{1,0:T(8,128)S(1)} %get-tuple-element.86), channel_id=1, source_target_pairs={{1,2},{2,1},{3,31},{5,6},{6,5},{7,27},{9,10},{10,9},{11,23},{13,14... | collective-permute-start | bytes 503816 | tf_op jit(solution)/shard_map/ppermute | solution.py:459
  6.8 6.9 %collective-permute-start.2 = (f32[24,128]{1,0:T(8,128)S(1)}, f32[24,128]{1,0:T(8,128)S(1)}, u32[]{:S(2)}, u32[]{:S(2)}) collective-permute-start(f32[24,128]{1,0:T(8,128)S(1)} %get-tuple-element.91), channel_id=1, source_target_pairs={{0,4},{4,8},{8,12},{12,16},{16,20},{20,24},{24,28},{28,0},{1,5},{5... | collective-permute-start | bytes 36872 | tf_op jit(solution)/shard_map/ppermute | solution.py:455
  7.0 6.7 %collective-permute-start.3 = (f32[24,128]{1,0:T(8,128)S(1)}, f32[24,128]{1,0:T(8,128)S(1)}, u32[]{:S(2)}, u32[]{:S(2)}) collective-permute-start(f32[24,128]{1,0:T(8,128)S(1)} %get-tuple-element.92), channel_id=1, source_target_pairs={{4,0},{8,4},{12,8},{16,12},{20,16},{24,20},{28,24},{0,28},{5,1},{9... | collective-permute-start | bytes 36872 | tf_op jit(solution)/shard_map/ppermute | solution.py:463

commit v6 on v5

--- a/solution.py
+++ b/solution.py
@@ -18,8 +18,8 @@
 LOADS = (0.5, 1.0)
 STORES = (0.2, 0.4, 0.6, 0.8, 1.0)
 UNROLL = 4
-EVEN = (2, 6)
-ODD = (5, 5)
+EVEN = (1, 5)
+ODD = (5, 6)
 
 
 def taper(slope):
@@ -165,7 +165,13 @@
 def middle_kernel(dims, x_ref, kmt_ref, *refs):
     *refs, turned_ref = refs
     refs = refs[len(refs) // 2 :]
-    inner_body(dims, *early_blocks(), turned_ref, x_ref, kmt_ref, *refs)
+    early, done = early_blocks()
+
+    @pl.when((early == 0) & (done > 0))
+    def _():
+        coefs_body(dims, x_ref, kmt_ref, *refs[2:])
+
+    inner_body(dims, early, done, turned_ref, x_ref, kmt_ref, *refs)
 
 
 def late_kernel(dims, x_ref, kmt_ref, *refs):
@@ -400,6 +406,12 @@
         copy.wait()
 
 
+def idle_partner(lon, lons):
+    if lons % 8 == 0 and (lon * 4 // lons) % 2 == 1:
+        return (lon + lons // 2) % lons
+    return lon ^ 1 if lons % 2 == 0 else lon
+
+
 def row_pairs(color, lons, lats):
     pairs = []
     for lon in range(lons):
@@ -412,7 +424,7 @@
     free_out = set(range(lons * lats)) - {a for a, _ in pairs}
     for target in free_in:
         lon, lat = divmod(target, lats)
-        source = (lon ^ 1 if lons % 2 == 0 else (lon + 1) % lons) * lats + lat
+        source = idle_partner(lon, lons) * lats + lat
         assert source in free_out
         pairs.append((source, target))
     return pairs

time: 15.3 us -> 15.3 us (level)
  no operation moved by 1% of the time
where the time goes in v6:
time: 15.3 us; the launch traced here: 15.2 us
  starting transfers between devices  9.15 us (60%)
  Pallas kernels  5.93 us (39%)
    pallas_call x6, Pallas kernels, call(): pl.pallas_call(functools.partial(kernel, dims), out_shape=out, in_specs=[...  5.93 us
    ppermute x1, starting transfers between devices, local(): from_odd = lax.ppermute(odd, ('lon', 'lat'), row_pairs(1, lons, lats))  4.25 us
    ppermute x1, starting transfers between devices, local(): from_east = lax.ppermute(west, 'lon', [(b, a) for a, b in ring])  3.91 us
    ppermute x1, starting transfers between devices, local(): from_even = lax.ppermute(even, ('lon', 'lat'), row_pairs(0, lons, lats))  0.74 us
  transfers between devices with their start and end apart: 4, of which 0 were waited for; matrix products, arithmetic and copies ran while one was open for 0% of the time, Pallas kernels for 18%

profile of v6, /device:TPU:5, one launch (start us, length us, event | category | flops | bytes accessed | tf_op | source)
XLA Modules:
  0.0 15.2 jit_solution(6935290320463474332)
XLA Ops:
  0.0 1.8 %shard_map.28 = (f32[2560,128]{1,0:T(8,128)S(1)}, f32[64,128]{1,0:T(8,128)S(1)}, f32[24,128]{1,0:T(8,128)S(1)}, f32[24,128]{1,0:T(8,128)S(1)}, f32[8,128]{1,0:T(...) custom-call(f32[2560,128]{1,0:T(8,128)} %bitcast.2, s32[8,128]{1,0:T(8,128)} %kmt_hbm.1), custom_call_target="tpu_custom_call" | custom-call | flops 1000000 | bytes 1000000 | tf_op jit(solution)/shard_map/pallas_call | solution.py:447
  1.8 0.7 %collective-permute-start = (f32[328,128]{1,0:T(8,128)S(1)}, f32[328,128]{1,0:T(8,128)S(1)}, u32[]{:S(2)}, u32[]{:S(2)}) collective-permute-start(f32[328,128]{1,0:T(8,128)S(1)} %get-tuple-element.85), channel_id=1, source_target_pairs={{0,1},{1,0},{2,3},{3,2},{4,5},{5,4},{6,7},{7,6},{8,9},{9,8},{10,11... | collective-permute-start | bytes 503816 | tf_op jit(solution)/shard_map/ppermute | solution.py:474
  2.5 4.2 %collective-permute-start.1 = (f32[328,128]{1,0:T(8,128)S(1)}, f32[328,128]{1,0:T(8,128)S(1)}, u32[]{:S(2)}, u32[]{:S(2)}) collective-permute-start(f32[328,128]{1,0:T(8,128)S(1)} %get-tuple-element.86), channel_id=1, source_target_pairs={{1,2},{2,1},{3,31},{5,6},{6,5},{7,27},{9,10},{10,9},{11,23},{13,14... | collective-permute-start | bytes 503816 | tf_op jit(solution)/shard_map/ppermute | solution.py:471
  6.8 0.3 %collective-permute-start.2 = (f32[24,128]{1,0:T(8,128)S(1)}, f32[24,128]{1,0:T(8,128)S(1)}, u32[]{:S(2)}, u32[]{:S(2)}) collective-permute-start(f32[24,128]{1,0:T(8,128)S(1)} %get-tuple-element.91), channel_id=1, source_target_pairs={{0,4},{4,8},{8,12},{12,16},{16,20},{20,24},{24,28},{28,0},{1,5},{5... | collective-permute-start | bytes 36872 | tf_op jit(solution)/shard_map/ppermute | solution.py:467
  7.0 3.9 %collective-permute-start.3 = (f32[24,128]{1,0:T(8,128)S(1)}, f32[24,128]{1,0:T(8,128)S(1)}, u32[]{:S(2)}, u32[]{:S(2)}) collective-permute-start(f32[24,128]{1,0:T(8,128)S(1)} %get-tuple-element.92), channel_id=1, source_target_pairs={{4,0},{8,4},{12,8},{16,12},{20,16},{24,20},{28,24},{0,28},{5,1},{9... | collective-permute-start | bytes 36872 | tf_op jit(solution)/shard_map/ppermute | solution.py:475
  10.9 2.4 %shard_map.31 = (f32[2560,128]{1,0:T(8,128)S(1)}, f32[2560,128]{1,0:T(8,128)S(1)}, f32[64,128]{1,0:T(8,128)S(1)}, f32[64,128]{1,0:T(8,128)S(1)}, f32[64,128]{1,0...) custom-call(f32[2560,128]{1,0:T(8,128)S(1)} %get-tuple-element.51.x_, ...), custom_call_target="tpu_custom_call", output_to_operand_aliasing={{0}: (2, {}), {1}: (3, {}), {2}: (4, {}), {3}: (5, {}), {4}... | custom-call | flops 10000000 | bytes 10000000 | tf_op jit(solution)/shard_map/pallas_call | solution.py:447
  13.3 0.0 collective-permute-done.even_ref
  13.3 0.0 collective-permute-done.1.odd_ref
  13.3 0.4 %shard_map.32.base_ref = f32[2560,128]{1,0:T(8,128)S(1)} custom-call(f32[2560,128]{1,0:T(8,128)S(1)} %get-tuple-element.51.x_ref, f32[8,128]{1,0:T(8,128)S(1)} %get-tuple-element.49.kmt_ref, f32[2560,128]{1,0:T(8,128)S(1)} %get-tuple-element.82.base_ref, f32[2560,128]{1,0:T(8,128)S(1)} %get-tuple-element.83.cy_ref, ...), custom_call_target="tpu_custom_call", output_to_operand_aliasing={{}: (2, {})} | custom-call | flops 1000000 | bytes 1000000 | tf_op jit(solution)/shard_map/pallas_call | solution.py:447
  13.7 0.0 collective-permute-done.2.from_west
  13.7 0.0 collective-permute-done.3.from_east
  13.7 1.4 %shard_map.33 = f32[2560,128]{1,0:T(8,128)} custom-call(f32[8,128]{1,0:T(8,128)S(1)} %get-tuple-element.49.kmt_ref, f32[64,128]{1,0:T(8,128)S(1)} %get-tuple-element.50.own_ref, f32[2560,128]{1,0:T(8,128)S(1)} %shard_map.32.base_ref, f32[64,128]{1,0:T(8,128)S(1)} %get-tuple-element.87.inner_ref, f32[64,128]{1,0:T(8,128)S(1)} %get-tuple-element.88.dense_ref, ...), custom_call_target="tpu_custom_call" | custom-call | flops 10000000 | bytes 10000000 | tf_op jit(solution)/shard_map/pallas_call | solution.py:447
  (2 shorter events, 0.0 us)
Async XLA Ops:
  1.8 11.5 %collective-permute-start = (f32[328,128]{1,0:T(8,128)S(1)}, f32[328,128]{1,0:T(8,128)S(1)}, u32[]{:S(2)}, u32[]{:S(2)}) collective-permute-start(f32[328,128]{1,0:T(8,128)S(1)} %get-tuple-element.85), channel_id=1, source_target_pairs={{0,1},{1,0},{2,3},{3,2},{4,5},{5,4},{6,7},{7,6},{8,9},{9,8},{10,11... | collective-permute-start | bytes 503816 | tf_op jit(solution)/shard_map/ppermute | solution.py:474
  2.5 10.8 %collective-permute-start.1 = (f32[328,128]{1,0:T(8,128)S(1)}, f32[328,128]{1,0:T(8,128)S(1)}, u32[]{:S(2)}, u32[]{:S(2)}) collective-permute-start(f32[328,128]{1,0:T(8,128)S(1)} %get-tuple-element.86), channel_id=1, source_target_pairs={{1,2},{2,1},{3,31},{5,6},{6,5},{7,27},{9,10},{10,9},{11,23},{13,14... | collective-permute-start | bytes 503816 | tf_op jit(solution)/shard_map/ppermute | solution.py:471
  6.8 6.9 %collective-permute-start.2 = (f32[24,128]{1,0:T(8,128)S(1)}, f32[24,128]{1,0:T(8,128)S(1)}, u32[]{:S(2)}, u32[]{:S(2)}) collective-permute-start(f32[24,128]{1,0:T(8,128)S(1)} %get-tuple-element.91), channel_id=1, source_target_pairs={{0,4},{4,8},{8,12},{12,16},{16,20},{20,24},{24,28},{28,0},{1,5},{5... | collective-permute-start | bytes 36872 | tf_op jit(solution)/shard_map/ppermute | solution.py:467
  7.0 6.7 %collective-permute-start.3 = (f32[24,128]{1,0:T(8,128)S(1)}, f32[24,128]{1,0:T(8,128)S(1)}, u32[]{:S(2)}, u32[]{:S(2)}) collective-permute-start(f32[24,128]{1,0:T(8,128)S(1)} %get-tuple-element.92), channel_id=1, source_target_pairs={{4,0},{8,4},{12,8},{16,12},{20,16},{24,20},{28,24},{0,28},{5,1},{9... | collective-permute-start | bytes 36872 | tf_op jit(solution)/shard_map/ppermute | solution.py:475

commit v7 on v6

--- a/solution.py
+++ b/solution.py
@@ -293,50 +293,50 @@
         lax.fori_loop(first, last, step, 0)
 
 
-def rows_kernel(dims, x_ref, kmt_ref, base_ref, cy_ref, sum_y_ref, even_ref, odd_ref, out_ref):
+def end_kernel(color, dims, x_ref, kmt_ref, base_ref, cy_ref, sum_y_ref, there_ref, out_ref):
     nt, nz, rows, cols, _ = dims
     odd, bottom, _ = position()
-    kmt = kmt_ref[...]
+    north = odd if color == 1 else jnp.logical_not(odd)
     flat = (nz, cols)
     level = rows_of(flat).astype(jnp.float32)
 
-    def ends(index):
-        a, b = even_ref[pl.ds(index, nz), :], odd_ref[pl.ds(index, nz), :]
-        return jnp.where(odd, a, b), jnp.where(odd, b, a)
-
-    def own_rows(ref, t):
-        start = t * nz * rows
-        return ref[pl.ds(start, nz, stride=rows), :], ref[pl.ds(start + rows - 1, nz, stride=rows), :]
-
-    ghost_kmts = ends(nt * nz)
-    ghost_kmts = jnp.where(bottom, 0.0, ghost_kmts[0]), ghost_kmts[1]
-    own_kmts = jnp.broadcast_to(kmt[:1], flat), jnp.broadcast_to(kmt[rows - 1 :], flat)
-    heats, salts = (own_rows(x_ref, 0), ends(0)), (own_rows(x_ref, 1), ends(nz))
-    sums_before = own_rows(sum_y_ref, 0)
-    end_coefs = []
-    for end, sign in ((0, -1.0), (1, 1.0)):
-        kmts = own_kmts[end], ghost_kmts[end]
-        wms = [as_mask(k > level + 1.0) for k in kmts]
+    def side(row, sign):
+        def own_row(ref, t):
+            return ref[pl.ds(t * nz * rows + row, nz, stride=rows), :]
+
+        def ghost_row(t):
+            return there_ref[pl.ds(t * nz, nz), :]
+
+        kmts = jnp.broadcast_to(kmt_ref[row : row + 1, :], flat), ghost_row(nt)
+        own_wm, ghost_wm = [as_mask(k > level + 1.0) for k in kmts]
         mask = as_mask(jnp.minimum(*kmts) > level)
-        densities = [density_of(h[end], s[end]) for h, s in zip(heats, salts)]
-        strats = [0.5 * level_rows(d, m)[1] for d, m in zip(densities, wms)]
-        slope = sign * slope_at(densities[1], densities[0], mask, *strats)
-        before = 0.25 * (sums_before[end] + pltpu.roll(sums_before[end], nz - 1, 0))
+        own_density = density_of(own_row(x_ref, 0), own_row(x_ref, 1))
+        ghost_density = density_of(ghost_row(0), ghost_row(1))
+        own_strat, ghost_strat = level_rows(own_density, own_wm)[1], level_rows(ghost_density, ghost_wm)[1]
+        slope = sign * slope_at(ghost_density, own_density, mask, 0.5 * own_strat, 0.5 * ghost_strat)
+        before = own_row(sum_y_ref, 0)
+        before = 0.25 * (before + pltpu.roll(before, nz - 1, 0))
         change = 0.25 * (slope + pltpu.roll(slope, nz - 1, 0))
         after = before + change
-        own_wm = wms[0]
-        end_coefs.append((wms, REDI * mask, sign * FACE * slope, sign * LEVEL * after * own_wm, LEVEL * change * own_wm,
-                          REDI * change * (before + after) * own_wm))
-    for t in range(nt):
-        for end in (0, 1):
-            wms, a, b, q, q_change, z_change = end_coefs[end]
-            here, there = own_rows(x_ref, t)[end], ends(t * nz)[end]
-            diff, own_sum = level_rows(here, wms[0])
+        a, b = REDI * mask, sign * FACE * slope
+        q, q_change = sign * LEVEL * after * own_wm, LEVEL * change * own_wm
+        z_change = REDI * change * (before + after) * own_wm
+        for t in range(nt):
+            here, there = own_row(x_ref, t), ghost_row(t)
+            diff, own_sum = level_rows(here, own_wm)
             grad = a * (there - here)
-            gain = grad + b * (own_sum + level_rows(there, wms[1])[1])
-            tilt = q * (grad + pltpu.roll(grad, nz - 1, 0)) + q_change * own_rows(cy_ref, t)[end] + z_change * diff
-            part = pl.ds(t * nz * rows + (rows - 1 if end else 0), nz, stride=rows)
+            gain = grad + b * (own_sum + level_rows(there, ghost_wm)[1])
+            tilt = q * (grad + pltpu.roll(grad, nz - 1, 0)) + q_change * own_row(cy_ref, t) + z_change * diff
+            part = pl.ds(t * nz * rows + row, nz, stride=rows)
             out_ref[part, :] = out_ref[part, :] + (gain + (tilt - pltpu.roll(tilt, 1, 0)))
+
+    @pl.when(north)
+    def _():
+        side(rows - 1, 1.0)
+
+    @pl.when(jnp.logical_not(north | bottom))
+    def _():
+        side(0, -1.0)
 
 
 def outer_kernel(dims, kmt_ref, own_ref, base_ref, inner_ref, dense_ref, cell_w_ref, cell_e_ref,
@@ -475,8 +475,9 @@
     from_east = lax.ppermute(west, "lon", [(b, a) for a, b in ring])
     inner = call(late_kernel, (near, near_kmt, *inner), shapes, turned, 10000000, aliases=aliases)
     base, cy, sum_y, inner_slope, dense, cell_w, cell_e = inner[:7]
-    ends = (near, near_kmt, base, cy, sum_y, from_even, from_odd)
-    (base,) = call(rows_kernel, ends, (block,), [], 1000000, aliases={2: 0})
+    for color, there in ((0, from_even), (1, from_odd)):
+        inputs = (near, near_kmt, base, cy, sum_y, there)
+        (base,) = call(functools.partial(end_kernel, color), inputs, (block,), [], 1000000, aliases={2: 0})
     out = call(
         outer_kernel,
         (near_kmt, own, base, inner_slope, dense, cell_w, cell_e, from_west, from_east),

time: 15.3 us -> 15.4 us (level)
    pallas_call x6 -> x7, Pallas kernels: 5.93 us -> 6.01 us  [call(): pl.pallas_call(functools.partial(kernel, dims), out_shape=out, in_specs=[...]
  transfers between devices with their start and end apart: 4 -> 4, of which waited for: 0 -> 0; matrix products, arithmetic and copies ran while one was open for 0% -> 0% of each run, Pallas kernels for 18% -> 19%
where the time goes in v7:
time: 15.4 us; the launch traced here: 15.2 us
  starting transfers between devices  9.15 us (59%)
  Pallas kernels  6.01 us (39%)
    pallas_call x7, Pallas kernels, call(): pl.pallas_call(functools.partial(kernel, dims), out_shape=out, in_specs=[...  6.01 us
    ppermute x1, starting transfers between devices, local(): from_odd = lax.ppermute(odd, ('lon', 'lat'), row_pairs(1, lons, lats))  4.25 us
    ppermute x1, starting transfers between devices, local(): from_east = lax.ppermute(west, 'lon', [(b, a) for a, b in ring])  3.91 us
    ppermute x1, starting transfers between devices, local(): from_even = lax.ppermute(even, ('lon', 'lat'), row_pairs(0, lons, lats))  0.74 us
  transfers between devices with their start and end apart: 4, of which 0 were waited for; matrix products, arithmetic and copies ran while one was open for 0% of the time, Pallas kernels for 19%

profile of v7, /device:TPU:5, one launch (start us, length us, event | category | flops | bytes accessed | tf_op | source)
XLA Modules:
  0.0 15.2 jit_solution(9775305356770792522)
XLA Ops:
  0.0 1.8 %shard_map.28 = (f32[2560,128]{1,0:T(8,128)S(1)}, f32[64,128]{1,0:T(8,128)S(1)}, f32[24,128]{1,0:T(8,128)S(1)}, f32[24,128]{1,0:T(8,128)S(1)}, f32[8,128]{1,0:T(...) custom-call(f32[2560,128]{1,0:T(8,128)} %bitcast.2, s32[8,128]{1,0:T(8,128)} %kmt_hbm.1), custom_call_target="tpu_custom_call" | custom-call | flops 1000000 | bytes 1000000 | tf_op jit(solution)/shard_map/pallas_call | solution.py:447
  1.8 0.7 %collective-permute-start = (f32[328,128]{1,0:T(8,128)S(1)}, f32[328,128]{1,0:T(8,128)S(1)}, u32[]{:S(2)}, u32[]{:S(2)}) collective-permute-start(f32[328,128]{1,0:T(8,128)S(1)} %get-tuple-element.85), channel_id=1, source_target_pairs={{0,1},{1,0},{2,3},{3,2},{4,5},{5,4},{6,7},{7,6},{8,9},{9,8},{10,11... | collective-permute-start | bytes 503816 | tf_op jit(solution)/shard_map/ppermute | solution.py:474
  2.5 4.2 %collective-permute-start.1 = (f32[328,128]{1,0:T(8,128)S(1)}, f32[328,128]{1,0:T(8,128)S(1)}, u32[]{:S(2)}, u32[]{:S(2)}) collective-permute-start(f32[328,128]{1,0:T(8,128)S(1)} %get-tuple-element.86), channel_id=1, source_target_pairs={{1,2},{2,1},{3,31},{5,6},{6,5},{7,27},{9,10},{10,9},{11,23},{13,14... | collective-permute-start | bytes 503816 | tf_op jit(solution)/shard_map/ppermute | solution.py:471
  6.8 0.3 %collective-permute-start.2 = (f32[24,128]{1,0:T(8,128)S(1)}, f32[24,128]{1,0:T(8,128)S(1)}, u32[]{:S(2)}, u32[]{:S(2)}) collective-permute-start(f32[24,128]{1,0:T(8,128)S(1)} %get-tuple-element.91), channel_id=1, source_target_pairs={{0,4},{4,8},{8,12},{12,16},{16,20},{20,24},{24,28},{28,0},{1,5},{5... | collective-permute-start | bytes 36872 | tf_op jit(solution)/shard_map/ppermute | solution.py:467
  7.0 3.9 %collective-permute-start.3 = (f32[24,128]{1,0:T(8,128)S(1)}, f32[24,128]{1,0:T(8,128)S(1)}, u32[]{:S(2)}, u32[]{:S(2)}) collective-permute-start(f32[24,128]{1,0:T(8,128)S(1)} %get-tuple-element.92), channel_id=1, source_target_pairs={{4,0},{8,4},{12,8},{16,12},{20,16},{24,20},{28,24},{0,28},{5,1},{9... | collective-permute-start | bytes 36872 | tf_op jit(solution)/shard_map/ppermute | solution.py:475
  10.9 2.4 %shard_map.31 = (f32[2560,128]{1,0:T(8,128)S(1)}, f32[2560,128]{1,0:T(8,128)S(1)}, f32[64,128]{1,0:T(8,128)S(1)}, f32[64,128]{1,0:T(8,128)S(1)}, f32[64,128]{1,0...) custom-call(f32[2560,128]{1,0:T(8,128)S(1)} %get-tuple-element.51.x_, ...), custom_call_target="tpu_custom_call", output_to_operand_aliasing={{0}: (2, {}), {1}: (3, {}), {2}: (4, {}), {3}: (5, {}), {4}... | custom-call | flops 10000000 | bytes 10000000 | tf_op jit(solution)/shard_map/pallas_call | solution.py:447
  13.3 0.0 collective-permute-done.there_ref
  13.3 0.2 %shard_map.32.base_ref = f32[2560,128]{1,0:T(8,128)S(1)} custom-call(f32[2560,128]{1,0:T(8,128)S(1)} %get-tuple-element.51.x_ref, f32[8,128]{1,0:T(8,128)S(1)} %get-tuple-element.49.kmt_ref, f32[2560,128]{1,0:T(8,128)S(1)} %get-tuple-element.82.base_ref, f32[2560,128]{1,0:T(8,128)S(1)} %get-tuple-element.83.cy_ref, ...), custom_call_target="tpu_custom_call", output_to_operand_aliasing={{}: (2, {})} | custom-call | flops 1000000 | bytes 1000000 | tf_op jit(solution)/shard_map/pallas_call | solution.py:447
  13.6 0.0 collective-permute-done.1.there_ref
  13.6 0.2 %shard_map.33.base_ref = f32[2560,128]{1,0:T(8,128)S(1)} custom-call(f32[2560,128]{1,0:T(8,128)S(1)} %get-tuple-element.51.x_ref, f32[8,128]{1,0:T(8,128)S(1)} %get-tuple-element.49.kmt_ref, f32[2560,128]{1,0:T(8,128)S(1)} %shard_map.32.base_ref, f32[2560,128]{1,0:T(8,128)S(1)} %get-tuple-element.83.cy_ref, ...), custom_call_target="tpu_custom_call", output_to_operand_aliasing={{}: (2, {})} | custom-call | flops 1000000 | bytes 1000000 | tf_op jit(solution)/shard_map/pallas_call | solution.py:447
  13.8 0.0 collective-permute-done.2.from_west
  13.8 0.0 collective-permute-done.3.from_east
  13.8 1.4 %shard_map.34 = f32[2560,128]{1,0:T(8,128)} custom-call(f32[8,128]{1,0:T(8,128)S(1)} %get-tuple-element.49.kmt_ref, f32[64,128]{1,0:T(8,128)S(1)} %get-tuple-element.50.own_ref, f32[2560,128]{1,0:T(8,128)S(1)} %shard_map.33.base_ref, f32[64,128]{1,0:T(8,128)S(1)} %get-tuple-element.87.inner_ref, f32[64,128]{1,0:T(8,128)S(1)} %get-tuple-element.88.dense_ref, ...), custom_call_target="tpu_custom_call" | custom-call | flops 10000000 | bytes 10000000 | tf_op jit(solution)/shard_map/pallas_call | solution.py:447
  (2 shorter events, 0.0 us)
Async XLA Ops:
  1.8 11.6 %collective-permute-start = (f32[328,128]{1,0:T(8,128)S(1)}, f32[328,128]{1,0:T(8,128)S(1)}, u32[]{:S(2)}, u32[]{:S(2)}) collective-permute-start(f32[328,128]{1,0:T(8,128)S(1)} %get-tuple-element.85), channel_id=1, source_target_pairs={{0,1},{1,0},{2,3},{3,2},{4,5},{5,4},{6,7},{7,6},{8,9},{9,8},{10,11... | collective-permute-start | bytes 503816 | tf_op jit(solution)/shard_map/ppermute | solution.py:474
  2.5 11.1 %collective-permute-start.1 = (f32[328,128]{1,0:T(8,128)S(1)}, f32[328,128]{1,0:T(8,128)S(1)}, u32[]{:S(2)}, u32[]{:S(2)}) collective-permute-start(f32[328,128]{1,0:T(8,128)S(1)} %get-tuple-element.86), channel_id=1, source_target_pairs={{1,2},{2,1},{3,31},{5,6},{6,5},{7,27},{9,10},{10,9},{11,23},{13,14... | collective-permute-start | bytes 503816 | tf_op jit(solution)/shard_map/ppermute | solution.py:471
  6.8 7.0 %collective-permute-start.2 = (f32[24,128]{1,0:T(8,128)S(1)}, f32[24,128]{1,0:T(8,128)S(1)}, u32[]{:S(2)}, u32[]{:S(2)}) collective-permute-start(f32[24,128]{1,0:T(8,128)S(1)} %get-tuple-element.91), channel_id=1, source_target_pairs={{0,4},{4,8},{8,12},{12,16},{16,20},{20,24},{24,28},{28,0},{1,5},{5... | collective-permute-start | bytes 36872 | tf_op jit(solution)/shard_map/ppermute | solution.py:467
  7.0 6.8 %collective-permute-start.3 = (f32[24,128]{1,0:T(8,128)S(1)}, f32[24,128]{1,0:T(8,128)S(1)}, u32[]{:S(2)}, u32[]{:S(2)}) collective-permute-start(f32[24,128]{1,0:T(8,128)S(1)} %get-tuple-element.92), channel_id=1, source_target_pairs={{4,0},{8,4},{12,8},{16,12},{20,16},{24,20},{28,24},{0,28},{5,1},{9... | collective-permute-start | bytes 36872 | tf_op jit(solution)/shard_map/ppermute | solution.py:475

commit v8 on v7

--- a/solution.py
+++ b/solution.py
@@ -16,7 +16,7 @@
 FACE = 0.25 * (REDI - SKEW)
 LEVEL = 0.25 * (REDI + SKEW) / REDI
 LOADS = (0.5, 1.0)
-STORES = (0.2, 0.4, 0.6, 0.8, 1.0)
+STORES = (0.1, 0.2, 0.3, 0.4, 0.5, 0.6, 0.7, 0.8, 0.9, 1.0)
 UNROLL = 4
 EVEN = (1, 5)
 ODD = (5, 6)
@@ -66,7 +66,7 @@
     return jnp.take_along_axis(values, index, axis=1, mode="promise_in_bounds")
 
 
-def pair_of(west, east, cols=128):
+def pair_of(west, east, cols):
     shape = (west.shape[0], cols)
     return jnp.where(lax.rem(lanes_of(shape), 2) == 0, jnp.broadcast_to(west, shape), jnp.broadcast_to(east, shape))
 
@@ -207,14 +207,14 @@
         ax_ref[part, :] = REDI * mask
         bx_ref[part, :] = FACE * slope
         sum_x.append(slope + pltpu.roll(slope, cols - 1, 1))
-        inner_ref[part, :] = pair_of(slope[:, 1:2], slope[:, cols - 1 :])
+        inner_ref[part, :] = pair_of(slope[:, 1:2], slope[:, cols - 1 :], cols)
         mask = as_mask(kmt_y > k)
         slope = slope_at(density[k], pltpu.roll(density[k], 1, 0), mask, strat[k], pltpu.roll(strat[k], 1, 0))
         ay_ref[part, :] = REDI * mask
         by_ref[part, :] = FACE * slope
         sum_y.append(slope + pltpu.roll(slope, rows - 1, 0))
         sum_y_ref[part, :] = sum_y[k]
-        dense_ref[part, :] = pair_of(density[k][:, :1], density[k][:, cols - 1 :])
+        dense_ref[part, :] = pair_of(density[k][:, :1], density[k][:, cols - 1 :], cols)
         cell_w_ref[part, :] = jnp.zeros(shape, jnp.float32)
         cell_e_ref[part, :] = jnp.zeros(shape, jnp.float32)
     for k in range(nz - 1):
@@ -353,12 +353,13 @@
 
     def spread(k, t):
         start = (k % per) * nt + t
-        return pair_of(load(from_west, k // per)[:, start : start + 1], load(from_east, k // per)[:, start : start + 1])
+        parts = (load(ref, k // per)[:, start : start + 1] for ref in (from_west, from_east))
+        return pair_of(*parts, cols)
 
     outward = jnp.where(even, -1.0, 1.0)
     own = [load(own_ref, k) for k in range(nz)]
     ghost = pairs_of(from_west, from_east, dims, nz)
-    own_kmt, ghost_kmt = pair_of(kmt[:, :1], kmt[:, cols - 1 :]), spread(nz, 0)
+    own_kmt, ghost_kmt = pair_of(kmt[:, :1], kmt[:, cols - 1 :], cols), spread(nz, 0)
     own_density = [load(dense_ref, k) for k in range(nz)]
     ghost_density = [density_of(spread(k, 0), spread(k, 1)) for k in range(nz)]
     own_wm = [as_mask(own_kmt > k + 1) for k in range(nz - 1)]
@@ -434,6 +435,7 @@
     nt, nz, rows, cols = tracers.shape
     lons, lats = lax.axis_size("lon"), lax.axis_size("lat")
     dims = (nt, nz, rows, cols, (lats - 1) % 2)
+    assert 2 * nt <= cols and nt % UNROLL == 0 and max(EVEN + ODD) <= nt // UNROLL
     packed = ((nz // (cols // nt) + 1) * rows, cols)
     edge = (nt * nz + nz, cols)
     level, block = (nz * rows, cols), (nt * nz * rows, cols)

time: 15.4 us -> 15.4 us (level)
  no operation moved by 1% of the time
where the time goes in v8:
time: 15.4 us; the launch traced here: 15.2 us
  starting transfers between devices  9.15 us (59%)
  Pallas kernels  6.02 us (39%)
    pallas_call x7, Pallas kernels, call(): pl.pallas_call(functools.partial(kernel, dims), out_shape=out, in_specs=[...  6.02 us
    ppermute x1, starting transfers between devices, local(): from_odd = lax.ppermute(odd, ('lon', 'lat'), row_pairs(1, lons, lats))  4.25 us
    ppermute x1, starting transfers between devices, local(): from_east = lax.ppermute(west, 'lon', [(b, a) for a, b in ring])  3.91 us
    ppermute x1, starting transfers between devices, local(): from_even = lax.ppermute(even, ('lon', 'lat'), row_pairs(0, lons, lats))  0.74 us
  transfers between devices with their start and end apart: 4, of which 0 were waited for; matrix products, arithmetic and copies ran while one was open for 0% of the time, Pallas kernels for 19%

profile of v8, /device:TPU:5, one launch (start us, length us, event | category | flops | bytes accessed | tf_op | source)
XLA Modules:
  0.0 15.2 jit_solution(11506530726398774990)
XLA Ops:
  0.0 1.8 %shard_map.28 = (f32[2560,128]{1,0:T(8,128)S(1)}, f32[64,128]{1,0:T(8,128)S(1)}, f32[24,128]{1,0:T(8,128)S(1)}, f32[24,128]{1,0:T(8,128)S(1)}, f32[8,128]{1,0:T(...) custom-call(f32[2560,128]{1,0:T(8,128)} %bitcast.2, s32[8,128]{1,0:T(8,128)} %kmt_hbm.1), custom_call_target="tpu_custom_call" | custom-call | flops 1000000 | bytes 1000000 | tf_op jit(solution)/shard_map/pallas_call | solution.py:449
  1.8 0.7 %collective-permute-start = (f32[328,128]{1,0:T(8,128)S(1)}, f32[328,128]{1,0:T(8,128)S(1)}, u32[]{:S(2)}, u32[]{:S(2)}) collective-permute-start(f32[328,128]{1,0:T(8,128)S(1)} %get-tuple-element.85), channel_id=1, source_target_pairs={{0,1},{1,0},{2,3},{3,2},{4,5},{5,4},{6,7},{7,6},{8,9},{9,8},{10,11... | collective-permute-start | bytes 503816 | tf_op jit(solution)/shard_map/ppermute | solution.py:476
  2.5 4.2 %collective-permute-start.1 = (f32[328,128]{1,0:T(8,128)S(1)}, f32[328,128]{1,0:T(8,128)S(1)}, u32[]{:S(2)}, u32[]{:S(2)}) collective-permute-start(f32[328,128]{1,0:T(8,128)S(1)} %get-tuple-element.86), channel_id=1, source_target_pairs={{1,2},{2,1},{3,31},{5,6},{6,5},{7,27},{9,10},{10,9},{11,23},{13,14... | collective-permute-start | bytes 503816 | tf_op jit(solution)/shard_map/ppermute | solution.py:473
  6.8 0.3 %collective-permute-start.2 = (f32[24,128]{1,0:T(8,128)S(1)}, f32[24,128]{1,0:T(8,128)S(1)}, u32[]{:S(2)}, u32[]{:S(2)}) collective-permute-start(f32[24,128]{1,0:T(8,128)S(1)} %get-tuple-element.91), channel_id=1, source_target_pairs={{0,4},{4,8},{8,12},{12,16},{16,20},{20,24},{24,28},{28,0},{1,5},{5... | collective-permute-start | bytes 36872 | tf_op jit(solution)/shard_map/ppermute | solution.py:469
  7.0 3.9 %collective-permute-start.3 = (f32[24,128]{1,0:T(8,128)S(1)}, f32[24,128]{1,0:T(8,128)S(1)}, u32[]{:S(2)}, u32[]{:S(2)}) collective-permute-start(f32[24,128]{1,0:T(8,128)S(1)} %get-tuple-element.92), channel_id=1, source_target_pairs={{4,0},{8,4},{12,8},{16,12},{20,16},{24,20},{28,24},{0,28},{5,1},{9... | collective-permute-start | bytes 36872 | tf_op jit(solution)/shard_map/ppermute | solution.py:477
  10.9 2.4 %shard_map.31 = (f32[2560,128]{1,0:T(8,128)S(1)}, f32[2560,128]{1,0:T(8,128)S(1)}, f32[64,128]{1,0:T(8,128)S(1)}, f32[64,128]{1,0:T(8,128)S(1)}, f32[64,128]{1,0...) custom-call(f32[2560,128]{1,0:T(8,128)S(1)} %get-tuple-element.51.x_, ...), custom_call_target="tpu_custom_call", output_to_operand_aliasing={{0}: (2, {}), {1}: (3, {}), {2}: (4, {}), {3}: (5, {}), {4}... | custom-call | flops 10000000 | bytes 10000000 | tf_op jit(solution)/shard_map/pallas_call | solution.py:449
  13.3 0.0 collective-permute-done.there_ref
  13.3 0.2 %shard_map.32.base_ref = f32[2560,128]{1,0:T(8,128)S(1)} custom-call(f32[2560,128]{1,0:T(8,128)S(1)} %get-tuple-element.51.x_ref, f32[8,128]{1,0:T(8,128)S(1)} %get-tuple-element.49.kmt_ref, f32[2560,128]{1,0:T(8,128)S(1)} %get-tuple-element.82.base_ref, f32[2560,128]{1,0:T(8,128)S(1)} %get-tuple-element.83.cy_ref, ...), custom_call_target="tpu_custom_call", output_to_operand_aliasing={{}: (2, {})} | custom-call | flops 1000000 | bytes 1000000 | tf_op jit(solution)/shard_map/pallas_call | solution.py:449
  13.6 0.0 collective-permute-done.1.there_ref
  13.6 0.2 %shard_map.33.base_ref = f32[2560,128]{1,0:T(8,128)S(1)} custom-call(f32[2560,128]{1,0:T(8,128)S(1)} %get-tuple-element.51.x_ref, f32[8,128]{1,0:T(8,128)S(1)} %get-tuple-element.49.kmt_ref, f32[2560,128]{1,0:T(8,128)S(1)} %shard_map.32.base_ref, f32[2560,128]{1,0:T(8,128)S(1)} %get-tuple-element.83.cy_ref, ...), custom_call_target="tpu_custom_call", output_to_operand_aliasing={{}: (2, {})} | custom-call | flops 1000000 | bytes 1000000 | tf_op jit(solution)/shard_map/pallas_call | solution.py:449
  13.8 0.0 collective-permute-done.2.from_west
  13.8 0.0 collective-permute-done.3.from_east
  13.8 1.4 %shard_map.34 = f32[2560,128]{1,0:T(8,128)} custom-call(f32[8,128]{1,0:T(8,128)S(1)} %get-tuple-element.49.kmt_ref, f32[64,128]{1,0:T(8,128)S(1)} %get-tuple-element.50.own_ref, f32[2560,128]{1,0:T(8,128)S(1)} %shard_map.33.base_ref, f32[64,128]{1,0:T(8,128)S(1)} %get-tuple-element.87.inner_ref, f32[64,128]{1,0:T(8,128)S(1)} %get-tuple-element.88.dense_ref, ...), custom_call_target="tpu_custom_call" | custom-call | flops 10000000 | bytes 10000000 | tf_op jit(solution)/shard_map/pallas_call | solution.py:449
  (2 shorter events, 0.0 us)
Async XLA Ops:
  1.8 11.6 %collective-permute-start = (f32[328,128]{1,0:T(8,128)S(1)}, f32[328,128]{1,0:T(8,128)S(1)}, u32[]{:S(2)}, u32[]{:S(2)}) collective-permute-start(f32[328,128]{1,0:T(8,128)S(1)} %get-tuple-element.85), channel_id=1, source_target_pairs={{0,1},{1,0},{2,3},{3,2},{4,5},{5,4},{6,7},{7,6},{8,9},{9,8},{10,11... | collective-permute-start | bytes 503816 | tf_op jit(solution)/shard_map/ppermute | solution.py:476
  2.5 11.1 %collective-permute-start.1 = (f32[328,128]{1,0:T(8,128)S(1)}, f32[328,128]{1,0:T(8,128)S(1)}, u32[]{:S(2)}, u32[]{:S(2)}) collective-permute-start(f32[328,128]{1,0:T(8,128)S(1)} %get-tuple-element.86), channel_id=1, source_target_pairs={{1,2},{2,1},{3,31},{5,6},{6,5},{7,27},{9,10},{10,9},{11,23},{13,14... | collective-permute-start | bytes 503816 | tf_op jit(solution)/shard_map/ppermute | solution.py:473
  6.8 7.0 %collective-permute-start.2 = (f32[24,128]{1,0:T(8,128)S(1)}, f32[24,128]{1,0:T(8,128)S(1)}, u32[]{:S(2)}, u32[]{:S(2)}) collective-permute-start(f32[24,128]{1,0:T(8,128)S(1)} %get-tuple-element.91), channel_id=1, source_target_pairs={{0,4},{4,8},{8,12},{12,16},{16,20},{20,24},{24,28},{28,0},{1,5},{5... | collective-permute-start | bytes 36872 | tf_op jit(solution)/shard_map/ppermute | solution.py:469
  7.0 6.8 %collective-permute-start.3 = (f32[24,128]{1,0:T(8,128)S(1)}, f32[24,128]{1,0:T(8,128)S(1)}, u32[]{:S(2)}, u32[]{:S(2)}) collective-permute-start(f32[24,128]{1,0:T(8,128)S(1)} %get-tuple-element.92), channel_id=1, source_target_pairs={{4,0},{8,4},{12,8},{16,12},{20,16},{24,20},{28,24},{0,28},{5,1},{9... | collective-permute-start | bytes 36872 | tf_op jit(solution)/shard_map/ppermute | solution.py:477
